TPU v7x, 32 devices: a whole 2x2x4 slice. The times are simulated.
32 devices in a mesh: gx: 8 (over z, y), gy: 4 (over x, core).
Axes of the slice: x: 2, y: 2, z: 4, core: 2. Of those that a mesh axis runs over, the one named last changes fastest.
Arguments:
- velocity: bfloat16 [3, 16, 16, 16, 512], P(None, 'gx', 'gy'), may hold values from -6 to 6
- part_pos: float32 [4096, 3, 128], P(('gx', 'gy')), may hold values from -1 to 1
- part_vel: float32 [4096, 3, 128], P(('gx', 'gy')), may hold values from -6 to 6
- part_coef: float32 [4096, 2, 128], P(('gx', 'gy')), may hold values from 0.3 to 3
- counts: int32 [4096], P(('gx', 'gy')), may hold values from 1 to 128
- dest: int32 [4096], P(('gx', 'gy')), may hold values from 0 to 3, as said below
- elem: int32 [4096], P(('gx', 'gy')), may hold values from 0 to 127, as said below
Outputs:
- drag: float32 [4096, 3, 128], P(('gx', 'gy'))
- source: float32 [3, 16, 16, 16, 512], P(None, 'gx', 'gy')
Inputs may be any that keep to these rules, and one draw needn't show every extreme that they name: `dest`: every device sends exactly 32 blocks to each gy index. `elem`: on every owning device, each of its 128 elements receives exactly one block.
All inputs are finite; a program needn't handle non-finite values.
Results may differ from a plain program's by a relative error of at most 0.0003.
Values sent between devices are 32-bit elements; how exact they have to be, the bound alone decides.
A program may use at most 128 MiB of HBM per device.

v0:
```python
import math

import jax
import jax.numpy as jnp
from jax import lax
from jax.sharding import PartitionSpec as P

GLL = (
    -1.0,
    -0.8717401485096066,
    -0.5917001814331423,
    -0.2092992179024789,
    0.2092992179024789,
    0.5917001814331423,
    0.8717401485096066,
    1.0,
)
HIGH = lax.Precision.HIGHEST
SHARPNESS = 8.0


def shifted(shard, axis, by):
    count = lax.axis_size(axis)
    pairs = [(i, i + by) for i in range(count) if 0 <= i + by < count]
    return lax.ppermute(shard, axis, pairs)


def lagrange_rows(coord):
    layers = []
    for i in range(8):
        product = jnp.ones_like(coord)
        for m in range(8):
            if m != i:
                product = product * ((coord - GLL[m]) / (GLL[i] - GLL[m]))
        layers.append(product)
    return jnp.stack(layers, axis=1)


def gauss_rows(coord, offset):
    points = jnp.array(GLL, dtype=jnp.float32)
    spacing = points[None, :, None] - (coord[:, None, :] + offset)
    return jnp.exp(-SHARPNESS * spacing * spacing)


def spread_rows(position, drag):
    group = position.shape[0]
    width = position.shape[2]
    weights_s = gauss_rows(position[:, 1], 0.0)
    weights_t = gauss_rows(position[:, 2], 0.0)
    spread = (
        (-drag)[:, :, None, None, :]
        * weights_s[:, None, :, None, :]
        * weights_t[:, None, None, :, :]
    )
    return spread.reshape(group, 3, 64, width)


def element_step(field, position, carried, coefs, filled):
    group = position.shape[0]
    width = position.shape[2]
    basis_r = lagrange_rows(position[:, 0])
    basis_s = lagrange_rows(position[:, 1])
    basis_t = lagrange_rows(position[:, 2])
    nodal = field.reshape(3, group, 8, 64)
    partial_sum = jnp.einsum("cgia,gip->gcap", nodal, basis_r, precision=HIGH)
    planes = (basis_s[:, :, None, :] * basis_t[:, None, :, :]).reshape(group, 64, width)
    fluid = jnp.sum(partial_sum * planes[:, None], axis=2)
    relative = fluid - carried
    speed = jnp.sqrt(jnp.sum(relative * relative, axis=1))
    factor = coefs[:, 0] * (1.0 + 0.15 * jnp.power(coefs[:, 1] * speed, 0.687))
    live = jnp.arange(width, dtype=jnp.int32)[None, :] < filled[:, None]
    drag = jnp.where(live[:, None, :], factor[:, None, :] * relative, jnp.zeros_like(relative))
    spread = spread_rows(position, drag)
    weights_r = jnp.stack(
        [
            gauss_rows(position[:, 0], 0.0),
            gauss_rows(position[:, 0], 2.0),
            gauss_rows(position[:, 0], -2.0),
        ],
        axis=0,
    )
    deposit = jnp.einsum("sgip,gcap->scgia", weights_r, spread, precision=HIGH)
    return (drag, deposit.reshape(3, 3, group, 512))


def run_groups(field, position, carried, coefs, filled, group):
    total = position.shape[0]
    turns = total // group
    drag_init = jnp.zeros(carried.shape, jnp.float32)
    deposit_init = jnp.zeros((3, 3, total, field.shape[2]), jnp.float32)

    def one_turn(index, state):
        drag_all, deposit_all = state
        start = index * group
        piece = lax.dynamic_slice_in_dim(field, start, group, 1).astype(jnp.float32)
        drag, deposit = element_step(
            piece,
            lax.dynamic_slice_in_dim(position, start, group, 0),
            lax.dynamic_slice_in_dim(carried, start, group, 0),
            lax.dynamic_slice_in_dim(coefs, start, group, 0),
            lax.dynamic_slice_in_dim(filled, start, group, 0),
        )
        drag_all = lax.dynamic_update_slice_in_dim(drag_all, drag, start, 0)
        deposit_all = lax.dynamic_update_slice_in_dim(deposit_all, deposit, start, 2)
        return (drag_all, deposit_all)

    return lax.fori_loop(0, turns, one_turn, (drag_init, deposit_init))


def dss_axis(field, elem_axis, node_axis, far_lo, far_hi):
    count = field.shape[elem_axis]
    lower = lax.slice_in_dim(field, 0, 1, axis=node_axis)
    upper = lax.slice_in_dim(field, 7, 8, axis=node_axis)
    edge_shape = lax.slice_in_dim(lower, 0, 1, axis=elem_axis).shape
    lower_next = jnp.concatenate(
        [lax.slice_in_dim(lower, 1, count, axis=elem_axis), far_lo.reshape(edge_shape)],
        axis=elem_axis,
    )
    upper_prev = jnp.concatenate(
        [far_hi.reshape(edge_shape), lax.slice_in_dim(upper, 0, count - 1, axis=elem_axis)],
        axis=elem_axis,
    )
    middle = lax.slice_in_dim(field, 1, 7, axis=node_axis)
    return jnp.concatenate([lower + upper_prev, middle, upper + lower_next], axis=node_axis)


def edge_face(field, elem_axis, elem_index, node_axis, node_index):
    edge = lax.slice_in_dim(field, elem_index, elem_index + 1, axis=elem_axis)
    return lax.slice_in_dim(edge, node_index, node_index + 1, axis=node_axis).reshape(-1)


def flat_layer(layer):
    return layer.reshape(layer.shape[:4] + (512,))


def cube_layer(layer):
    return layer.reshape(layer.shape[:4] + (8, 8, 8))


def body(velocity, part_pos, part_vel, part_coef, counts, dest, elem):
    exd, eyd, ez, nodes = (
        velocity.shape[1],
        velocity.shape[2],
        velocity.shape[3],
        velocity.shape[4],
    )
    total_elems = exd * eyd * ez
    sorting = jnp.argsort(dest, stable=True)
    inverse = jnp.argsort(sorting)
    labels = jnp.stack([counts, elem], axis=1).astype(jnp.float32)
    sent = (part_pos[sorting], part_vel[sorting], part_coef[sorting], labels[sorting])
    got_pos, got_vel, got_coef, got_labels = (
        lax.all_to_all(sent[0], "gy", split_axis=0, concat_axis=0, tiled=True),
        lax.all_to_all(sent[1], "gy", split_axis=0, concat_axis=0, tiled=True),
        lax.all_to_all(sent[2], "gy", split_axis=0, concat_axis=0, tiled=True),
        lax.all_to_all(sent[3], "gy", split_axis=0, concat_axis=0, tiled=True),
    )
    elem_got = got_labels[:, 1].astype(jnp.int32)
    count_got = got_labels[:, 0].astype(jnp.int32)
    by_elem = jnp.argsort(elem_got)
    field_flat = velocity.reshape(3, total_elems, nodes)
    sorted_places = got_pos[by_elem]
    drag_e, deposit = run_groups(
        field_flat,
        sorted_places,
        got_vel[by_elem],
        got_coef[by_elem],
        count_got[by_elem],
        math.gcd(total_elems, 32),
    )
    returned = lax.all_to_all(drag_e[elem_got], "gy", split_axis=0, concat_axis=0, tiled=True)
    drag_out = returned[inverse]
    deposit = deposit.reshape(3, 3, exd, eyd, ez, 8, 8, 8)
    own_part, minus_part, plus_part = (deposit[0], deposit[1], deposit[2])
    empty_layer = jnp.zeros_like(own_part[:, 0:1])
    empty_rest = jnp.zeros_like(own_part[:, 1:])
    inside = (
        own_part
        + jnp.concatenate([minus_part[:, 1:], empty_layer], axis=1)
        + jnp.concatenate([empty_layer, plus_part[:, :-1]], axis=1)
    )
    minus_next = shifted(flat_layer(minus_part[:, 0:1]), "gx", -1)
    plus_prev = shifted(flat_layer(plus_part[:, -1:]), "gx", 1)
    total = (
        inside
        + jnp.concatenate([cube_layer(plus_prev), empty_rest], axis=1)
        + jnp.concatenate([empty_rest, cube_layer(minus_next)], axis=1)
    )
    far_lo = shifted(edge_face(total, 1, 0, 4, 0), "gx", -1)
    far_hi = shifted(edge_face(total, 1, exd - 1, 4, 7), "gx", 1)
    field = dss_axis(total, 1, 4, far_lo, far_hi)
    far_lo_y = shifted(edge_face(field, 2, 0, 5, 0), "gy", -1)
    far_hi_y = shifted(edge_face(field, 2, eyd - 1, 5, 7), "gy", 1)
    field = dss_axis(field, 2, 5, far_lo_y, far_hi_y)
    zeros_edge = jnp.zeros_like(edge_face(field, 3, 0, 6, 0))
    field = dss_axis(field, 3, 6, zeros_edge, zeros_edge)
    return (drag_out, field.reshape(3, exd, eyd, ez, nodes))


def solution(mesh):
    in_specs = (
        P(None, "gx", "gy", None, None),
        P(("gx", "gy"), None, None),
        P(("gx", "gy"), None, None),
        P(("gx", "gy"), None, None),
        P(("gx", "gy")),
        P(("gx", "gy")),
        P(("gx", "gy")),
    )
    out_specs = (P(("gx", "gy"), None, None), P(None, "gx", "gy", None, None))
    return jax.shard_map(body, mesh=mesh, in_specs=in_specs, out_specs=out_specs, check_vma=False)
```

profile of v0, /device:TPU:17, one launch (start us, length us, event | category | flops | bytes accessed | tf_op | source)
XLA Modules:
  0.0 237.1 jit_solution(3717806881338690757)
XLA Ops:
  0.7 3.2 %sort.48 = (s32[128]{0:T(128)}, s32[128]{0:T(128)S(1)}) sort(s32[128]{0:T(128)} %param.19, s32[128]{0:T(128)S(1)} %iota.26), dimensions={0}, to_apply=%region_0.0 | sort | flops 896 | bytes 2048 | tf_op jit(solution)/shard_map/jit(argsort)/sort | solution.py:148
  6.0 3.9 %all-to-all-start = ((f32[4,32,2]{1,2,0:T(2,128)}), f32[4,32,2]{1,2,0:T(2,128)S(1)}, u32[]{:S(2)}, u32[]{:S(2)}) async-start(f32[4,32,2]{1,2,0:T(2,128)} %copy.144), calls=%async_computation | async-start | bytes 8192 | tf_op jit(solution)/shard_map/all_to_all | solution.py:156
  13.0 4.0 %all-to-all-start.1 = ((f32[128,2,128]{2,1,0:T(2,128)}), f32[128,2,128]{2,1,0:T(2,128)S(1)}, u32[]{:S(2)}, u32[]{:S(2)}) async-start(f32[128,2,128]{2,1,0:T(2,128)} %gather_fusion.2), calls=%async_computation.1 | async-start | bytes 262144 | tf_op jit(solution)/shard_map/all_to_all | solution.py:155
  23.1 3.4 %all-to-all-start.2 = ((f32[128,3,128]{2,1,0:T(4,128)}), f32[128,3,128]{2,1,0:T(4,128)S(1)}, u32[]{:S(2)}, u32[]{:S(2)}) async-start(f32[128,3,128]{2,1,0:T(4,128)} %copy.146), calls=%async_computation.2 | async-start | bytes 524288 | tf_op jit(solution)/shard_map/all_to_all | solution.py:153
  31.6 4.7 %all-to-all-start.3 = ((f32[128,3,128]{2,1,0:T(4,128)}), f32[128,3,128]{2,1,0:T(4,128)S(1)}, u32[]{:S(2)}, u32[]{:S(2)}) async-start(f32[128,3,128]{2,1,0:T(4,128)} %copy.147), calls=%async_computation.3 | async-start | bytes 524288 | tf_op jit(solution)/shard_map/all_to_all | solution.py:154
  43.8 49.8 %while.20 = (s32[]{:T(128)}, f32[128,3,128]{2,1,0:T(4,128)S(1)}, f32[3,3,128,512]{3,2,1,0:T(8,128)}, s32[128]{0:T(128)S(1)}, f32[128,2,128]{2,1,0:T(2,128)S(1)},...) while((s32[]{:T(128)}, f32[128,3,128]{2,1,0:T(4,128)S(1)}, ...), condition=%wide.region_5.6_spmd.clone.clone, body=%wide.region_2.5_spmd.sunk.clone.clone.sunk | while | flops 307449856 | bytes 12215059 | solution.py:107
  48.2 6.6 %fusion.52 = f32[3,3,32,8,64]{4,3,0,1,2:T(8,128)S(1)} fusion(f32[32,64,128]{2,1,0:T(8,128)S(1)} %broadcast_bitcast_fusion.2, f32[32,3,8,128]{3,2,1,0:T(8,128)S(1)} %broadcast_multiply_fusion.2, f32[1,32,8,128]{3,2,0,1:T(8,128)S(1)} %get-tuple-element.683, f32[1,32,8,128]{3,2,0,1:T(8,128)S(1)} %get-tuple-element.684, ...), kind=kOutput, calls=%fused_computation.16.clone.1 | convolution fusion | flops 227475456 | bytes 2424832 | tf_op jit(solution)/shard_map/while/body/eval_jaxpr/sgip,gcap->scgia/dot_general | solution.py:82
  60.6 6.6 %fusion.52 = f32[3,3,32,8,64]{4,3,0,1,2:T(8,128)S(1)} fusion(f32[32,64,128]{2,1,0:T(8,128)S(1)} %broadcast_bitcast_fusion.2, f32[32,3,8,128]{3,2,1,0:T(8,128)S(1)} %broadcast_multiply_fusion.2, f32[1,32,8,128]{3,2,0,1:T(8,128)S(1)} %get-tuple-element.683, f32[1,32,8,128]{3,2,0,1:T(8,128)S(1)} %get-tuple-element.684, ...), kind=kOutput, calls=%fused_computation.16.clone.1 | convolution fusion | flops 227475456 | bytes 2424832 | tf_op jit(solution)/shard_map/while/body/eval_jaxpr/sgip,gcap->scgia/dot_general | solution.py:82
  73.1 6.6 %fusion.52 = f32[3,3,32,8,64]{4,3,0,1,2:T(8,128)S(1)} fusion(f32[32,64,128]{2,1,0:T(8,128)S(1)} %broadcast_bitcast_fusion.2, f32[32,3,8,128]{3,2,1,0:T(8,128)S(1)} %broadcast_multiply_fusion.2, f32[1,32,8,128]{3,2,0,1:T(8,128)S(1)} %get-tuple-element.683, f32[1,32,8,128]{3,2,0,1:T(8,128)S(1)} %get-tuple-element.684, ...), kind=kOutput, calls=%fused_computation.16.clone.1 | convolution fusion | flops 227475456 | bytes 2424832 | tf_op jit(solution)/shard_map/while/body/eval_jaxpr/sgip,gcap->scgia/dot_general | solution.py:82
  85.5 6.6 %fusion.52 = f32[3,3,32,8,64]{4,3,0,1,2:T(8,128)S(1)} fusion(f32[32,64,128]{2,1,0:T(8,128)S(1)} %broadcast_bitcast_fusion.2, f32[32,3,8,128]{3,2,1,0:T(8,128)S(1)} %broadcast_multiply_fusion.2, f32[1,32,8,128]{3,2,0,1:T(8,128)S(1)} %get-tuple-element.683, f32[1,32,8,128]{3,2,0,1:T(8,128)S(1)} %get-tuple-element.684, ...), kind=kOutput, calls=%fused_computation.16.clone.1 | convolution fusion | flops 227475456 | bytes 2424832 | tf_op jit(solution)/shard_map/while/body/eval_jaxpr/sgip,gcap->scgia/dot_general | solution.py:82
  93.6 2.9 %fusion.36 = (f32[1,3,128,512]{3,2,1,0:T(8,128)}, f32[1,3,128,512]{3,2,1,0:T(8,128)S(1)}, f32[1,3,128,512]{3,2,1,0:T(8,128)S(1)}) fusion(f32[3,3,128,512]{3,2,1,0:T(8,128)} %get-tuple-element.400), kind=kLoop, calls=%fused_computation.122 | loop fusion | bytes 4718592 | tf_op jit(solution)/shard_map/slice | solution.py:174
  97.9 16.2 %squeeze.27 = f32[3,2,4,16,8,8,8]{3,2,1,6,5,4,0:T(4,128)} reshape(f32[1,3,128,512]{2,3,1,0:T(8,128)S(1)} %copy.151) | data formatting | bytes 1572864 | tf_op jit(solution)/shard_map/squeeze | solution.py:174
  114.1 6.8 %fusion.34 = (f32[3,1,4,16,8,8,8]{3,2,1,6,5,4,0:T(4,128)}, f32[3,1,4,16,8,8,8]{3,2,1,6,5,4,0:T(4,128)S(1)}) fusion(f32[3,2,4,16,8,8,8]{3,2,1,6,5,4,0:T(4,128)} %squeeze.27), kind=kLoop, calls=%fused_computation.120 | loop fusion | bytes 1572864 | tf_op jit(solution)/shard_map/slice | solution.py:179
  123.0 3.0 %collective-permute-start.1 = (f32[3,1,4,16,512]{4,3,2,1,0:T(8,128)}, f32[3,1,4,16,512]{4,3,2,1,0:T(8,128)}, u32[]{:S(2)}, u32[]{:S(2)}) collective-permute-start(f32[3,1,4,16,512]{4,3,2,1,0:T(8,128)} %copy.158), channel_id=1, source_target_pairs={{4,0},{8,4},{12,8},{16,12},{20,16},{24,20},{28,24},{5,1},{9,5},{13... | collective-permute-start | bytes 1179656 | tf_op jit(solution)/shard_map/ppermute | solution.py:25
  126.0 6.6 %squeeze.28 = f32[3,2,4,16,8,8,8]{3,2,1,6,5,4,0:T(4,128)} reshape(f32[1,3,128,512]{2,3,1,0:T(8,128)} %copy.152) | data formatting | bytes 1572864 | tf_op jit(solution)/shard_map/squeeze | solution.py:174
  132.5 6.7 %fusion.35 = (f32[3,1,4,16,8,8,8]{3,2,1,6,5,4,0:T(4,128)}, f32[3,1,4,16,8,8,8]{3,2,1,6,5,4,0:T(4,128)S(1)}) fusion(f32[3,2,4,16,8,8,8]{3,2,1,6,5,4,0:T(4,128)} %squeeze.28), kind=kLoop, calls=%fused_computation.121 | loop fusion | bytes 1572864 | tf_op jit(solution)/shard_map/slice | solution.py:180
  147.4 5.5 %all-to-all-start.4 = ((f32[128,3,128]{2,1,0:T(4,128)}), f32[128,3,128]{2,1,0:T(4,128)}, u32[]{:S(2)}, u32[]{:S(2)}) async-start(f32[128,3,128]{2,1,0:T(4,128)} %gather_fusion.8), calls=%async_computation.4 | async-start | bytes 524288 | tf_op jit(solution)/shard_map/all_to_all | solution.py:171
  153.0 5.6 %squeeze.26 = f32[3,2,4,16,8,8,8]{3,2,1,6,5,4,0:T(4,128)} reshape(f32[1,3,128,512]{2,3,1,0:T(8,128)S(1)} %copy.150) | data formatting | bytes 1572864 | tf_op jit(solution)/shard_map/squeeze | solution.py:174
  158.6 3.1 %copy.159 = f32[3,1,4,16,512]{3,4,2,0,1:T(8,128)} copy(f32[3,1,4,16,512]{4,3,2,1,0:T(8,128)} %collective-permute-done.1) | data formatting | bytes 786432 | tf_op jit(solution)/shard_map/ppermute | solution.py:25
  161.7 4.4 %copy.160 = f32[3,1,4,16,8,8,8]{3,2,1,6,5,4,0:T(4,128)S(1)} copy(f32[3,1,4,16,8,8,8]{3,6,5,4,2,0,1:T(8,128)} %bitcast.128) | data formatting | bytes 786432 | tf_op jit(solution)/shard_map/reshape | solution.py:137
  166.1 3.1 %copy.155 = f32[3,1,4,16,512]{3,4,2,0,1:T(8,128)} copy(f32[3,1,4,16,512]{4,3,2,1,0:T(8,128)} %collective-permute-done) | data formatting | bytes 786432 | tf_op jit(solution)/shard_map/ppermute | solution.py:25
  169.2 4.5 %copy.156 = f32[3,1,4,16,8,8,8]{3,2,1,6,5,4,0:T(4,128)S(1)} copy(f32[3,1,4,16,8,8,8]{3,6,5,4,2,0,1:T(8,128)} %bitcast.129) | data formatting | bytes 786432 | tf_op jit(solution)/shard_map/reshape | solution.py:137
  173.7 5.5 %pad_add_fusion = f32[3,2,4,16,8,8,8]{3,2,1,6,5,4,0:T(4,128)S(1)} fusion(f32[3,1,4,16,8,8,8]{3,2,1,6,5,4,0:T(4,128)S(1)} %copy.160, f32[3,1,4,16,8,8,8]{3,2,1,6,5,4,0:T(4,128)S(1)} %copy.156, f32[3,1,4,16,8,8,8]{3,2,1,6,5,4,0:T(4,128)S(1)} %copy-done.6, f32[3,2,4,16,8,8,8]{3,2,1,6,5,4,0:T(4,128)} %squeeze.26, f32[3,1,4,16,8,8,8]{3,2,1,6,5,4,0:T(4,128)S(1)} %copy-done.5), kind=kLoop, calls=%fused_computation.86 | loop fusion | flops 786432 | bytes 3145728 | tf_op jit(solution)/shard_map/add | solution.py:185
  179.3 2.6 %copy-done.3 = f32[3,2,4,16,8,8,8]{3,2,1,6,5,4,0:T(4,128)} copy-done((f32[3,2,4,16,8,8,8]{3,2,1,6,5,4,0:T(4,128)}, f32[3,2,4,16,8,8,8]{3,2,1,6,5,4,0:T(4,128)S(1)}, u32[]{:S(2)}) %copy-start.3) | copy-done | bytes 786456
  183.1 4.0 %collective-permute-start.2 = (f32[12288]{0:T(1024)S(1)}, f32[12288]{0:T(1024)S(1)}, u32[]{:S(2)}, u32[]{:S(2)}) collective-permute-start(f32[12288]{0:T(1024)S(1)} %reshape.216), channel_id=1, source_target_pairs={{0,4},{4,8},{8,12},{12,16},{16,20},{20,24},{24,28},{1,5},{5,9},{9,... | collective-permute-start | bytes 147464 | tf_op jit(solution)/shard_map/ppermute | solution.py:25
  192.6 6.4 %slice.231 = f32[3,2,4,16,6,8,8]{3,2,1,6,5,4,0:T(4,128)} slice(f32[3,2,4,16,8,8,8]{3,2,1,6,5,4,0:T(4,128)} %copy-done.3), slice={[0:3], [0:2], [0:4], [0:16], [1:7], [0:8], [0:8]} | slice | bytes 1179648 | tf_op jit(solution)/shard_map/slice | solution.py:123
  205.1 4.1 %collective-permute-start.4 = (f32[6144]{0:T(1024)S(1)}, f32[6144]{0:T(1024)S(1)}, u32[]{:S(2)}, u32[]{:S(2)}) collective-permute-start(f32[6144]{0:T(1024)S(1)} %reshape.220), channel_id=1, source_target_pairs={{0,1},{1,2},{2,3},{4,5},{5,6},{6,7},{8,9},{9,10},{10,11},{12,13},{... | collective-permute-start | bytes 73736 | tf_op jit(solution)/shard_map/ppermute | solution.py:25
  211.6 3.9 %pad_maximum_fusion = f32[3,2,4,16,8,8,8]{3,2,1,6,5,4,0:T(4,128)S(1)} fusion(f32[3,2,4,16,1,8,8]{3,2,1,6,5,4,0:T(4,128)S(1)} %get-tuple-element.545, f32[3,2,4,16,6,8,8]{3,2,1,6,5,4,0:T(4,128)} %slice.231, f32[3,2,4,16,1,8,8]{3,2,1,6,5,4,0:T(4,128)S(1)} %get-tuple-element.544), kind=kLoop, calls=%fused_computation.83 | loop fusion | flops 393216 | bytes 1572864 | tf_op jit(solution)/shard_map/concatenate | solution.py:124
  215.5 3.1 %slice.235 = f32[3,2,4,16,8,6,8]{3,2,1,6,5,4,0:T(4,128)} slice(f32[3,2,4,16,8,8,8]{3,2,1,6,5,4,0:T(4,128)S(1)} %pad_maximum_fusion), slice={[0:3], [0:2], [0:4], [0:16], [0:8], [1:7], [0:8]} | slice | bytes 1179648 | tf_op jit(solution)/shard_map/slice | solution.py:123
  219.5 2.7 %fusion.31 = (f32[3,2,4,16,8,1,8]{3,2,1,6,5,4,0:T(4,128)S(1)}, f32[3,2,4,16,8,1,8]{3,2,1,6,5,4,0:T(4,128)S(1)}) fusion(f32[3,2,4,16,1,8,8]{3,2,1,6,5,4,0:T(4,128)S(1)} %get-tuple-element.545, f32[3,2,4,16,6,8,8]{3,2,1,6,5,4,0:T(4,128)} %slice.231, f32[3,2,4,16,1,8,8]{3,2,1,6,5,4,0:T(4,128)S(1)} %get-tuple-element.544, ...), kind=kLoop, calls=%fused_computation.101 | loop fusion | flops 294912 | bytes 1032192 | tf_op jit(solution)/shard_map/add | solution.py:124
  226.8 3.9 %pad_maximum_fusion.2 = f32[3,2,4,16,8,8,8]{3,2,1,6,5,4,0:T(4,128)} fusion(f32[3,2,4,16,8,8,1]{3,2,1,6,5,4,0:T(4,128)S(1)} %get-tuple-element.539, f32[3,2,4,16,8,8,6]{3,2,1,6,5,4,0:T(4,128)S(1)} %slice.236, f32[3,2,4,16,8,8,1]{3,2,1,6,5,4,0:T(4,128)S(1)} %get-tuple-element.538), kind=kLoop, calls=%fused_computation.85 | loop fusion | flops 393216 | bytes 1572864 | tf_op jit(solution)/shard_map/concatenate | solution.py:124
  230.7 6.1 %copy.171 = f32[3,2,4,16,512]{4,3,2,1,0:T(8,128)} copy(f32[3,2,4,16,512]{3,2,1,4,0:T(4,128)} %bitcast.127) | data formatting | bytes 1572864
  (206 shorter events, 78.7 us)
Async XLA Ops:
  0.6 18.9 %copy-start = (f32[128,3,128]{2,0,1:T(8,128)S(1)}, f32[128,3,128]{2,0,1:T(8,128)}, u32[]{:S(2)}) copy-start(f32[128,3,128]{2,0,1:T(8,128)} %param.16) | copy-start | bytes 589828
  0.6 20.6 %copy-start.4 = (f32[128,3,128]{2,0,1:T(8,128)S(1)}, f32[128,3,128]{2,0,1:T(8,128)}, u32[]{:S(2)}) copy-start(f32[128,3,128]{2,0,1:T(8,128)} %param.15) | copy-start | bytes 589828
  6.0 7.0 %all-to-all-start = ((f32[4,32,2]{1,2,0:T(2,128)}), f32[4,32,2]{1,2,0:T(2,128)S(1)}, u32[]{:S(2)}, u32[]{:S(2)}) async-start(f32[4,32,2]{1,2,0:T(2,128)} %copy.144), calls=%async_computation | async-start | bytes 8192 | tf_op jit(solution)/shard_map/all_to_all | solution.py:156
  13.0 10.1 %all-to-all-start.1 = ((f32[128,2,128]{2,1,0:T(2,128)}), f32[128,2,128]{2,1,0:T(2,128)S(1)}, u32[]{:S(2)}, u32[]{:S(2)}) async-start(f32[128,2,128]{2,1,0:T(2,128)} %gather_fusion.2), calls=%async_computation.1 | async-start | bytes 262144 | tf_op jit(solution)/shard_map/all_to_all | solution.py:155
  20.4 23.4 %copy-start.8 = (f32[8]{0:T(128)S(1)}, f32[8]{0:T(128)}, u32[]{:S(2)}) copy-start(f32[8]{0:T(128)} %constant.1101.clone..sunk.11) | copy-start | bytes 100
  23.1 8.5 %all-to-all-start.2 = ((f32[128,3,128]{2,1,0:T(4,128)}), f32[128,3,128]{2,1,0:T(4,128)S(1)}, u32[]{:S(2)}, u32[]{:S(2)}) async-start(f32[128,3,128]{2,1,0:T(4,128)} %copy.146), calls=%async_computation.2 | async-start | bytes 524288 | tf_op jit(solution)/shard_map/all_to_all | solution.py:153
  31.6 9.7 %all-to-all-start.3 = ((f32[128,3,128]{2,1,0:T(4,128)}), f32[128,3,128]{2,1,0:T(4,128)S(1)}, u32[]{:S(2)}, u32[]{:S(2)}) async-start(f32[128,3,128]{2,1,0:T(4,128)} %copy.147), calls=%async_computation.3 | async-start | bytes 524288 | tf_op jit(solution)/shard_map/all_to_all | solution.py:154
  93.6 4.3 %copy-start.7 = (f32[128,3,128]{2,1,0:T(4,128)}, f32[128,3,128]{2,1,0:T(4,128)S(1)}, u32[]{:S(2)}) copy-start(f32[128,3,128]{2,1,0:T(4,128)S(1)} %get-tuple-element.398) | copy-start | bytes 589828
  123.0 35.6 %collective-permute-start.1 = (f32[3,1,4,16,512]{4,3,2,1,0:T(8,128)}, f32[3,1,4,16,512]{4,3,2,1,0:T(8,128)}, u32[]{:S(2)}, u32[]{:S(2)}) collective-permute-start(f32[3,1,4,16,512]{4,3,2,1,0:T(8,128)} %copy.158), channel_id=1, source_target_pairs={{4,0},{8,4},{12,8},{16,12},{20,16},{24,20},{28,24},{5,1},{9,5},{13... | collective-permute-start | bytes 1179656 | tf_op jit(solution)/shard_map/ppermute | solution.py:25
  141.4 24.7 %collective-permute-start = (f32[3,1,4,16,512]{4,3,2,1,0:T(8,128)}, f32[3,1,4,16,512]{4,3,2,1,0:T(8,128)}, u32[]{:S(2)}, u32[]{:S(2)}) collective-permute-start(f32[3,1,4,16,512]{4,3,2,1,0:T(8,128)} %copy.154), channel_id=1, source_target_pairs={{0,4},{4,8},{8,12},{12,16},{16,20},{20,24},{24,28},{1,5},{5,9},{9,... | collective-permute-start | bytes 1179656 | tf_op jit(solution)/shard_map/ppermute | solution.py:25
  147.4 42.8 %all-to-all-start.4 = ((f32[128,3,128]{2,1,0:T(4,128)}), f32[128,3,128]{2,1,0:T(4,128)}, u32[]{:S(2)}, u32[]{:S(2)}) async-start(f32[128,3,128]{2,1,0:T(4,128)} %gather_fusion.8), calls=%async_computation.4 | async-start | bytes 524288 | tf_op jit(solution)/shard_map/all_to_all | solution.py:171
  169.2 4.6 %copy-start.5 = (f32[3,1,4,16,8,8,8]{3,2,1,6,5,4,0:T(4,128)S(1)}, f32[3,1,4,16,8,8,8]{3,2,1,6,5,4,0:T(4,128)}, u32[]{:S(2)}) copy-start(f32[3,1,4,16,8,8,8]{3,2,1,6,5,4,0:T(4,128)} %get-tuple-element.550) | copy-start | bytes 1179652
  169.2 4.6 %copy-start.6 = (f32[3,1,4,16,8,8,8]{3,2,1,6,5,4,0:T(4,128)S(1)}, f32[3,1,4,16,8,8,8]{3,2,1,6,5,4,0:T(4,128)}, u32[]{:S(2)}) copy-start(f32[3,1,4,16,8,8,8]{3,2,1,6,5,4,0:T(4,128)} %get-tuple-element.552) | copy-start | bytes 1179652
  179.3 2.7 %copy-start.3 = (f32[3,2,4,16,8,8,8]{3,2,1,6,5,4,0:T(4,128)}, f32[3,2,4,16,8,8,8]{3,2,1,6,5,4,0:T(4,128)S(1)}, u32[]{:S(2)}) copy-start(f32[3,2,4,16,8,8,8]{3,2,1,6,5,4,0:T(4,128)S(1)} %pad_add_fusion) | copy-start | bytes 2359300
  183.1 15.9 %collective-permute-start.2 = (f32[12288]{0:T(1024)S(1)}, f32[12288]{0:T(1024)S(1)}, u32[]{:S(2)}, u32[]{:S(2)}) collective-permute-start(f32[12288]{0:T(1024)S(1)} %reshape.216), channel_id=1, source_target_pairs={{0,4},{4,8},{8,12},{12,16},{16,20},{20,24},{24,28},{1,5},{5,9},{9,... | collective-permute-start | bytes 147464 | tf_op jit(solution)/shard_map/ppermute | solution.py:25
  187.9 11.9 %collective-permute-start.3 = (f32[12288]{0:T(1024)S(1)}, f32[12288]{0:T(1024)S(1)}, u32[]{:S(2)}, u32[]{:S(2)}) collective-permute-start(f32[12288]{0:T(1024)S(1)} %reshape.218), channel_id=1, source_target_pairs={{4,0},{8,4},{12,8},{16,12},{20,16},{24,20},{28,24},{5,1},{9,5},{13... | collective-permute-start | bytes 147464 | tf_op jit(solution)/shard_map/ppermute | solution.py:25
  201.3 2.9 %copy-start.2 = (f32[3,2,4,16,6,8,8]{3,2,1,6,5,4,0:T(4,128)S(1)}, f32[3,2,4,16,6,8,8]{3,2,1,6,5,4,0:T(4,128)}, u32[]{:S(2)}) copy-start(f32[3,2,4,16,6,8,8]{3,2,1,6,5,4,0:T(4,128)} %slice.231) | copy-start | bytes 1769476
  205.1 13.5 %collective-permute-start.4 = (f32[6144]{0:T(1024)S(1)}, f32[6144]{0:T(1024)S(1)}, u32[]{:S(2)}, u32[]{:S(2)}) collective-permute-start(f32[6144]{0:T(1024)S(1)} %reshape.220), channel_id=1, source_target_pairs={{0,1},{1,2},{2,3},{4,5},{5,6},{6,7},{8,9},{9,10},{10,11},{12,13},{... | collective-permute-start | bytes 73736 | tf_op jit(solution)/shard_map/ppermute | solution.py:25
  209.6 9.4 %collective-permute-start.5 = (f32[6144]{0:T(1024)S(1)}, f32[6144]{0:T(1024)S(1)}, u32[]{:S(2)}, u32[]{:S(2)}) collective-permute-start(f32[6144]{0:T(1024)S(1)} %reshape.222), channel_id=1, source_target_pairs={{1,0},{2,1},{3,2},{5,4},{6,5},{7,6},{9,8},{10,9},{11,10},{13,12},{... | collective-permute-start | bytes 73736 | tf_op jit(solution)/shard_map/ppermute | solution.py:25
  219.1 3.2 %slice-start = ((s8[4718592]{0:T(1024)(128)(4,1)}), s8[524288]{0:T(1024)(128)(4,1)S(1)}, s32[]{:S(2)}) async-start(s8[4718592]{0:T(1024)(128)(4,1)} %bitcast.125), calls=%async_computation.5 | async-start | bytes 1048576
  219.5 3.0 %slice-start.1 = ((s8[4718592]{0:T(1024)(128)(4,1)}), s8[4194304]{0:T(1024)(128)(4,1)S(1)}, s32[]{:S(2)}) async-start(s8[4718592]{0:T(1024)(128)(4,1)} %bitcast.125), calls=%async_computation.6 | async-start | bytes 8388608
  226.8 10.1 %copy-start.1 = (f32[128,3,128]{2,0,1:T(8,128)S(1)}, f32[128,3,128]{2,0,1:T(8,128)}, u32[]{:S(2)}) copy-start(f32[128,3,128]{2,0,1:T(8,128)} %param.16) | copy-start | bytes 589828
where the time goes:
time: 236 us; the launch traced here: 237 us
  local copies, waits for them, and re-layouts  122 us (52%)
  starting transfers between devices  39.2 us (17%)
  other arithmetic  35.2 us (15%)
  matrix products  33.3 us (14%)
  waiting for transfers between devices  5.54 us (2%)
    squeeze x3, local copies, waits for them, and re-layouts, body(): own_part, minus_part, plus_part = (deposit[0], deposit[1], deposit[2])  28.3 us
    dot_general x4, matrix products, element_step(): deposit = jnp.einsum('sgip,gcap->scgia', weights_r, spread, precision=HIGH)  26.4 us
    ppermute x6, starting transfers between devices, shifted(): return lax.ppermute(shard, axis, pairs)  17.6 us
    slice x3, local copies, waits for them, and re-layouts, dss_axis(): middle = lax.slice_in_dim(field, 1, 7, axis=node_axis)  10.7 us
    unnamed x25, local copies, waits for them, and re-layouts  10.5 us
    concatenate x3, other arithmetic, dss_axis(): jnp.concatenate([lower + upper_prev, middle, upper + lower_next], axis=no...  9.6 us
    reshape x2, local copies, waits for them, and re-layouts, cube_layer(): return layer.reshape(layer.shape[:4] + (8, 8, 8))  8.94 us
    dot_general x4, matrix products, element_step(): partial_sum = jnp.einsum('cgia,gip->gcap', nodal, basis_r, precision=HIGH)  6.91 us
  transfers between devices with their start and end apart: 11, of which 3 were waited for; matrix products, arithmetic and copies ran while one was open for 33% of the time, Pallas kernels for 0%

commit v1 on v0

v1 whole, which is shorter than its diff:
```python
import functools

import jax
import jax.numpy as jnp
from jax import lax
from jax.experimental import pallas as pl
from jax.experimental.pallas import tpu as pltpu
from jax.sharding import PartitionSpec as P

GLL = (
    -1.0,
    -0.8717401485096066,
    -0.5917001814331423,
    -0.2092992179024789,
    0.2092992179024789,
    0.5917001814331423,
    0.8717401485096066,
    1.0,
)
SHARPNESS = 8.0
VMEM = pltpu.VMEM
SMEM = pltpu.SMEM
ROWS = 24


def lane_iota(shape):
    return lax.broadcasted_iota(jnp.int32, shape, len(shape) - 1)


def node_consts():
    row = lax.broadcasted_iota(jnp.int32, (8, 128), 0)

    def pick(values):
        out = jnp.full((8, 128), values[7], jnp.float32)
        for i in range(7):
            out = jnp.where(row == i, jnp.float32(values[i]), out)
        return out

    others = [pick([[GLL[m] for m in range(8) if m != i][n] for i in range(8)]) for n in range(7)]
    scales = []
    for i in range(8):
        product = 1.0
        for m in range(8):
            if m != i:
                product *= GLL[i] - GLL[m]
        scales.append(1.0 / product)
    return pick(GLL), others, pick(scales)


def lagrange(x, others, scale):
    diffs = [x - o for o in others]
    left = (diffs[0] * diffs[1]) * (diffs[2] * diffs[3])
    right = (diffs[4] * diffs[5]) * (diffs[6] * scale)
    return left * right


def gauss(x, nodes):
    gap = nodes - x
    return jnp.exp(-SHARPNESS * gap * gap)


def split(x):
    high = x.astype(jnp.bfloat16)
    low = (x - high.astype(jnp.float32)).astype(jnp.bfloat16)
    return high, low


def planes(a, b):
    return jnp.concatenate([a[j : j + 1] * b for j in range(8)], axis=0)


def spread_nodes(vel_ref, vs_ref, elems):
    low = lane_iota((elems, 128)) < 64
    for c in range(3):
        for q in range(4):
            x = vel_ref[c, :, q * 128 : (q + 1) * 128].astype(jnp.float32)
            turned = pltpu.roll(x, 64, 1)
            vs_ref[pl.ds(c * 8 + 2 * q, elems, stride=ROWS), :] = jnp.where(low, x, turned)
            vs_ref[pl.ds(c * 8 + 2 * q + 1, elems, stride=ROWS), :] = jnp.where(low, turned, x)


def element(block, count, field, consts):
    nodes, others, scale = consts
    r, s, t = (jnp.broadcast_to(block[d : d + 1], (8, 128)) for d in range(3))
    basis_r = lagrange(r, others, scale)
    basis_st = planes(lagrange(s, others, scale), lagrange(t, others, scale))
    high, low = split(basis_st)
    partial = jnp.dot(
        field.astype(jnp.bfloat16),
        jnp.concatenate([high, low], axis=0),
        preferred_element_type=jnp.float32,
    )
    rel = []
    for c in range(3):
        fluid = jnp.sum(partial[c * 8 : c * 8 + 8] * basis_r, axis=0, keepdims=True)
        rel.append(fluid - block[3 + c : 4 + c])
    speed = jnp.sqrt(rel[0] * rel[0] + rel[1] * rel[1] + rel[2] * rel[2])
    power = jnp.exp(0.687 * jnp.log(block[7:8] * speed))
    factor = block[6:7] * (1.0 + 0.15 * power)
    factor = jnp.where(lane_iota((1, 128)) < count, factor, 0.0)
    drag = [factor * w for w in rel]
    g_high, g_low = split(planes(gauss(s, nodes), gauss(t, nodes)))
    gathered = jnp.concatenate([g_high, g_low], axis=0)
    weights = [gauss(r, nodes), gauss(r + 2.0, nodes), gauss(r - 2.0, nodes)]
    left = jnp.concatenate([(-d) * w for w in weights for d in drag], axis=0)
    l_high, l_low = split(left)
    deposit = lax.dot_general(
        jnp.concatenate([l_high, l_low], axis=1),
        jnp.concatenate([gathered, gathered], axis=1),
        (((1,), (1,)), ((), ())),
        preferred_element_type=jnp.float32,
    )
    return jnp.concatenate(drag, axis=0), deposit


def compute_kernel(
    exd, slot_ref, count_ref, got_ref, vel_ref,
    drag_ref, total_ref, prev_ref, next_ref,
    vs_ref, ts_ref, gm_ref, gp_ref,
):
    elems = vel_ref.shape[1]
    columns = elems // exd
    group = 4 if columns % 4 == 0 else 1
    spread_nodes(vel_ref, vs_ref, elems)
    consts = node_consts()

    def turn(index, carry):
        for g in range(group):
            col = index * group + g
            deposits = []
            for x in range(exd):
                e = x * columns + col
                slot = slot_ref[e]
                drag, deposit = element(
                    got_ref[slot],
                    count_ref[slot],
                    vs_ref[pl.ds(pl.multiple_of(e * ROWS, 8), ROWS), :],
                    consts,
                )
                drag_ref[slot] = drag
                deposits.append(deposit)
            for x in range(exd):
                e = x * columns + col
                own = deposits[x][0:ROWS]
                if x + 1 < exd:
                    own = own + deposits[x + 1][ROWS : 2 * ROWS]
                if x > 0:
                    own = own + deposits[x - 1][2 * ROWS :]
                ts_ref[pl.ds(pl.multiple_of(e * ROWS, 8), ROWS), :] = own
            start = pl.multiple_of(col * ROWS, 8)
            gm_ref[pl.ds(start, ROWS), :] = deposits[0][ROWS : 2 * ROWS]
            gp_ref[pl.ds(start, ROWS), :] = deposits[exd - 1][2 * ROWS :]
        return carry

    lax.fori_loop(0, columns // group, turn, 0)

    def lanes(src, count, c, q):
        low = lane_iota((count, 128)) < 64
        even = src[pl.ds(c * 8 + 2 * q, count, stride=ROWS), :]
        odd = src[pl.ds(c * 8 + 2 * q + 1, count, stride=ROWS), :]
        mine = jnp.where(low, even, odd)
        other = jnp.where(low, odd, even)
        return mine + pltpu.roll(other, 64, 1)

    for c in range(3):
        for q in range(4):
            spot = slice(q * 128, (q + 1) * 128)
            total = lanes(ts_ref, elems, c, q)
            total_ref[c, :, spot] = total
            prev_ref[c, :, spot] = lanes(gm_ref, columns, c, q)
            next_ref[c, :, spot] = lanes(gp_ref, columns, c, q)
            if q == 0:
                prev_ref[c, :, 512:640] = total[0:columns]
            if q == 3:
                next_ref[c, :, 512:640] = total[elems - columns :]


def run_compute(slot, count, got, velocity, exd):
    elems = velocity.shape[1]
    columns = elems // exd
    f32 = jnp.float32
    return pl.pallas_call(
        functools.partial(compute_kernel, exd),
        out_shape=(
            jax.ShapeDtypeStruct((elems, 3, 128), f32),
            jax.ShapeDtypeStruct((3, elems, 512), f32),
            jax.ShapeDtypeStruct((3, columns, 640), f32),
            jax.ShapeDtypeStruct((3, columns, 640), f32),
        ),
        in_specs=[
            pl.BlockSpec(memory_space=SMEM),
            pl.BlockSpec(memory_space=SMEM),
            pl.BlockSpec(memory_space=VMEM),
            pl.BlockSpec(memory_space=VMEM),
        ],
        out_specs=[pl.BlockSpec(memory_space=VMEM)] * 4,
        scratch_shapes=[
            pltpu.VMEM((elems * ROWS, 128), f32),
            pltpu.VMEM((elems * ROWS, 128), f32),
            pltpu.VMEM((columns * ROWS, 128), f32),
            pltpu.VMEM((columns * ROWS, 128), f32),
        ],
        compiler_params=pltpu.CompilerParams(vmem_limit_bytes=48 * 1024 * 1024),
        cost_estimate=pl.CostEstimate(flops=200_000_000, bytes_accessed=4_000_000, transcendentals=700_000),
        name="elements",
    )(slot, count, got, velocity)


def x_pass(total_ref, prev_ref, next_ref, from_prev, from_next, field_ref, lo_ref, hi_ref):
    _, exd, eyd, ez, _ = total_ref.shape
    at = lax.axis_index("gx")
    first = jnp.where(at > 0, 1.0, 0.0)
    last = jnp.where(at < lax.axis_size("gx") - 1, 1.0, 0.0)
    low = lane_iota((ez, 128)) < 64
    place = lane_iota((ez, 128)) % 64

    def column(c, y):
        rows = slice(y * ez, (y + 1) * ez)
        grid = []
        for x in range(exd):
            quads = []
            for q in range(4):
                spot = slice(q * 128, (q + 1) * 128)
                v = total_ref[c, x, y, :, spot]
                if x == 0:
                    v = v + from_prev[c, rows, spot] * first
                if x == exd - 1:
                    v = v + from_next[c, rows, spot] * last
                quads.append(v)
            grid.append(quads)
        far_lo = (from_next[c, rows, 512:640] + next_ref[c, rows, 0:128]) * last
        far_hi = (from_prev[c, rows, 512:640] + prev_ref[c, rows, 384:512]) * first
        for x in range(exd):
            above = grid[x + 1][0] if x + 1 < exd else far_lo
            below = grid[x - 1][3] if x > 0 else far_hi
            done = list(grid[x])
            done[3] = done[3] + jnp.where(low, 0.0, pltpu.roll(above, 64, 1))
            done[0] = done[0] + jnp.where(low, pltpu.roll(below, 64, 1), 0.0)
            for q in range(4):
                field_ref[c, x, y, :, q * 128 : (q + 1) * 128] = done[q]
            if y == 0:
                face = jnp.where(place < 8, done[0], 0.0)
                for q in range(1, 4):
                    face = face + pltpu.roll(jnp.where(place < 8, done[q], 0.0), 8 * q, 1)
                lo_ref[c, x] = face
            if y == eyd - 1:
                face = jnp.where(place >= 56, done[0], 0.0)
                for q in range(1, 4):
                    face = face + pltpu.roll(jnp.where(place >= 56, done[q], 0.0), 128 - 8 * q, 1)
                hi_ref[c, x] = face

    for c in range(3):
        for y in range(eyd):
            column(c, y)


def yz_pass(field_ref, far_lo_ref, far_hi_ref, out_ref):
    _, exd, eyd, ez, _ = field_ref.shape
    at = lax.axis_index("gy")
    first = jnp.where(at > 0, 1.0, 0.0)
    last = jnp.where(at < lax.axis_size("gy") - 1, 1.0, 0.0)
    place = lane_iota((ez, 128)) % 64
    k = lane_iota((ez, 128)) % 8
    row = lax.broadcasted_iota(jnp.int32, (ez, 128), 0)
    up = (k == 7) & (row < ez - 1)
    down = (k == 0) & (row > 0)
    for c in range(3):
        for x in range(exd):
            far_lo = far_lo_ref[c, x] * last
            far_hi = far_hi_ref[c, x] * first
            for q in range(4):
                spot = slice(q * 128, (q + 1) * 128)
                cells = [field_ref[c, x, y, :, spot] for y in range(eyd)]
                for y in range(eyd):
                    if y + 1 < eyd:
                        above = pltpu.roll(cells[y + 1], 56, 1)
                    else:
                        above = pltpu.roll(far_lo, (56 - 8 * q) % 128, 1)
                    if y > 0:
                        below = pltpu.roll(cells[y - 1], 72, 1)
                    else:
                        below = pltpu.roll(far_hi, (72 + 8 * q) % 128, 1)
                    v = cells[y] + jnp.where(place >= 56, above, 0.0) + jnp.where(place < 8, below, 0.0)
                    nxt = pltpu.roll(pltpu.roll(v, ez - 1, 0), 7, 1)
                    prv = pltpu.roll(pltpu.roll(v, 1, 0), 121, 1)
                    out_ref[c, x, y, :, spot] = v + jnp.where(up, nxt, 0.0) + jnp.where(down, prv, 0.0)


def run_local(body, outs, *args, name):
    return pl.pallas_call(
        body,
        out_shape=outs,
        in_specs=[pl.BlockSpec(memory_space=VMEM)] * len(args),
        out_specs=jax.tree.map(lambda _: pl.BlockSpec(memory_space=VMEM), outs),
        compiler_params=pltpu.CompilerParams(vmem_limit_bytes=48 * 1024 * 1024),
        name=name,
    )(*args)


def shifted(shard, axis, by):
    count = lax.axis_size(axis)
    pairs = [(i, i + by) for i in range(count) if 0 <= i + by < count]
    return lax.ppermute(shard, axis, pairs)


def inverse_of(position):
    n = position.shape[0]
    ladder = jnp.arange(n, dtype=jnp.int32)
    return jnp.sum(jnp.where(position[None, :] == ladder[:, None], ladder[None, :], 0), axis=1)


def body(velocity, part_pos, part_vel, part_coef, counts, dest, elem):
    _, exd, eyd, ez, nodes = velocity.shape
    elems = exd * eyd * ez
    devices = lax.axis_size("gy")
    share = elems // devices
    f32 = jnp.float32
    ladder = jnp.arange(elems, dtype=jnp.int32)
    earlier = (dest[None, :] == dest[:, None]) & (ladder[None, :] < ladder[:, None])
    position = dest * share + jnp.sum(earlier.astype(jnp.int32), axis=1)
    sorting = inverse_of(position)
    packed = jnp.concatenate([part_pos, part_vel, part_coef], axis=1)[sorting]
    labels = (elem * 256 + counts)[sorting].astype(f32)
    got = lax.all_to_all(packed, "gy", split_axis=0, concat_axis=0, tiled=True)
    got_labels = lax.all_to_all(labels.reshape(devices, share), "gy", split_axis=0, concat_axis=0, tiled=True)
    got_labels = got_labels.reshape(elems).astype(jnp.int32)
    slot = inverse_of(got_labels // 256)
    drag_slots, total, to_prev, to_next = run_compute(
        slot, got_labels % 256, got, velocity.reshape(3, elems, nodes), exd
    )
    returned = lax.all_to_all(drag_slots, "gy", split_axis=0, concat_axis=0, tiled=True)
    drag_out = returned[position]
    from_next = shifted(to_prev, "gx", -1)
    from_prev = shifted(to_next, "gx", 1)
    cube = jax.ShapeDtypeStruct((3, exd, eyd, ez, nodes), f32)
    face = jax.ShapeDtypeStruct((3, exd, ez, 128), f32)
    field, lo, hi = run_local(
        x_pass, (cube, face, face),
        total.reshape(cube.shape), to_prev, to_next, from_prev, from_next, name="xpass",
    )
    far_lo = shifted(lo, "gy", -1)
    far_hi = shifted(hi, "gy", 1)
    source = run_local(yz_pass, cube, field, far_lo, far_hi, name="yzpass")
    return (drag_out, source)


def solution(mesh):
    in_specs = (
        P(None, "gx", "gy", None, None),
        P(("gx", "gy"), None, None),
        P(("gx", "gy"), None, None),
        P(("gx", "gy"), None, None),
        P(("gx", "gy")),
        P(("gx", "gy")),
        P(("gx", "gy")),
    )
    out_specs = (P(("gx", "gy"), None, None), P(None, "gx", "gy", None, None))
    return jax.shard_map(body, mesh=mesh, in_specs=in_specs, out_specs=out_specs, check_vma=False)
```

time: 236 us -> 82.8 us (0.35); the launches traced: 237 us -> 81.3 us
  local copies, waits for them, and re-layouts: 122 us -> 8.41 us
  other arithmetic: 35.2 us -> 1.37 us
  matrix products: 33.3 us -> 0 us
  Pallas kernels: 0 us -> 24.5 us
  waiting for transfers between devices: 5.54 us -> 22.3 us
  starting transfers between devices: 39.2 us -> 23.9 us
    dot_general x8 -> x0, matrix products: 33.3 us -> none  [the longest x4 26.4 us: element_step(): deposit = jnp.einsum('sgip,gcap->scgia', weights_r, spread, precision=HIGH)]
    slice x18 -> x0, local copies, waits for them, and re-layouts: 31.6 us -> none  [the longest x3 10.7 us: dss_axis(): middle = lax.slice_in_dim(field, 1, 7, axis=node_axis)]
    squeeze x3 -> x0, local copies, waits for them, and re-layouts: 28.3 us -> none  [body(): own_part, minus_part, plus_part = (deposit[0], deposit[1], deposit[2])]
    pallas_call x0 -> x3, Pallas kernels: none -> 24.5 us  [the longest x1 16.4 us: run_compute(): pl.pallas_call(functools.partial(compute_kernel, exd), out_shape=(jax.Sha...]
    reshape x24 -> x0, local copies, waits for them, and re-layouts: 19.8 us -> none  [the longest x2 8.94 us: cube_layer(): return layer.reshape(layer.shape[:4] + (8, 8, 8))]
    ppermute x6 -> x4, waiting for transfers between devices: 0.02 us -> 14.7 us  [shifted(): return lax.ppermute(shard, axis, pairs)]
    add x4 -> x1, other arithmetic: 11.8 us -> 0.01 us  [body(): labels = (elem * 256 + counts)[sorting].astype(f32)]
    gather x12 -> x3, local copies, waits for them, and re-layouts: 13.9 us -> 4.49 us  [the longest x1 1.71 us: body(): drag_out = returned[position]]
  transfers between devices with their start and end apart: 11 -> 7, of which waited for: 3 -> 3; matrix products, arithmetic and copies ran while one was open for 33% -> 6% of each run, Pallas kernels for 0% -> 1%
where the time goes in v1:
time: 82.8 us; the launch traced here: 81.3 us
  Pallas kernels  24.5 us (30%)
  starting transfers between devices  23.9 us (29%)
  waiting for transfers between devices  22.3 us (27%)
  local copies, waits for them, and re-layouts  8.41 us (10%)
  other arithmetic  1.37 us (2%)
    pallas_call x1, Pallas kernels, run_compute(): pl.pallas_call(functools.partial(compute_kernel, exd), out_shape=(jax.Sha...  16.4 us
    ppermute x4, waiting for transfers between devices, shifted(): return lax.ppermute(shard, axis, pairs)  14.7 us
    ppermute x4, starting transfers between devices, shifted(): return lax.ppermute(shard, axis, pairs)  10.8 us
    pallas_call x2, Pallas kernels, run_local(): pl.pallas_call(body, out_shape=outs, in_specs=[pl.BlockSpec(memory_space=...  8.1 us
    all_to_all x1, waiting for transfers between devices, body(): got = lax.all_to_all(packed, 'gy', split_axis=0, concat_axis=0, tiled=True)  7.62 us
    all_to_all x1, starting transfers between devices, body(): lax.all_to_all(drag_slots, 'gy', split_axis=0, concat_axis=0, tiled=True)  5.54 us
    all_to_all x1, starting transfers between devices, body(): lax.all_to_all(labels.reshape(devices, share), 'gy', split_axis=0, concat...  3.86 us
    all_to_all x1, starting transfers between devices, body(): got = lax.all_to_all(packed, 'gy', split_axis=0, concat_axis=0, tiled=True)  3.71 us
  transfers between devices with their start and end apart: 7, of which 3 were waited for; matrix products, arithmetic and copies ran while one was open for 6% of the time, Pallas kernels for 1%

profile of v1, /device:TPU:17, one launch (start us, length us, event | category | flops | bytes accessed | tf_op | source)
XLA Modules:
  0.0 81.3 jit_solution(15752852021474174773)
XLA Ops:
  0.6 0.9 %convert_reduce_fusion = s32[128]{0:T(128)S(1)} fusion(s32[128]{0:T(128)} %param.12), kind=kLoop, calls=%fused_computation.8 | loop fusion | flops 81792 | bytes 1024 | tf_op jit(solution)/shard_map/reduce_sum | solution.py:320
  1.6 0.1 select_reduce_fusion.1
  1.7 0.0 copy-start.5
  1.7 0.0 copy-start.6
  1.7 0.6 copy-done.5
  2.4 0.0 copy-done.6
  2.4 1.2 %gather_fusion = s32[128]{0:T(128)S(1)} fusion(s32[128]{0:T(128)S(1)} %multiply_add_fusion.1, s32[1024]{0:T(1024)S(1)} %pad_clamp_fusion.1), kind=kCustom, calls=%fused_computation | custom fusion | bytes 1536 | tf_op jit(solution)/shard_map/gather | solution.py:323
  3.6 0.7 convert_element_type.29
  4.3 3.9 %all-to-all-start = ((f32[4,1,32]{2,1,0:T(1,128)}), f32[4,1,32]{2,1,0:T(1,128)S(1)}, u32[]{:S(2)}, u32[]{:S(2)}) async-start(f32[4,1,32]{2,1,0:T(1,128)} %bitcast.2), calls=%async_computation | async-start | bytes 4096 | tf_op jit(solution)/shard_map/all_to_all | solution.py:325
  8.2 0.1 copy.19
  8.3 0.8 copy-done.2
  9.1 0.1 copy.20
  9.2 0.8 copy-done.3
  10.0 0.2 pad_maximum_fusion
  10.2 1.6 %gather_fusion.1 = f32[128,8,128]{2,1,0:T(8,128)} fusion(f32[128,8,128]{2,1,0:T(8,128)S(1)} %pad_maximum_fusion, s32[1024]{0:T(1024)S(1)} %pad_clamp_fusion.1), kind=kCustom, calls=%fused_computation.1 | custom fusion | bytes 1049088 | tf_op jit(solution)/shard_map/gather | solution.py:322
  11.7 0.0 all-to-all-done
  11.7 3.7 %all-to-all-start.1 = ((f32[128,8,128]{2,1,0:T(8,128)}), f32[128,8,128]{2,1,0:T(8,128)S(1)}, u32[]{:S(2)}, u32[]{:S(2)}) async-start(f32[128,8,128]{2,1,0:T(8,128)} %gather_fusion.1), calls=%async_computation.1 | async-start | bytes 1048576 | tf_op jit(solution)/shard_map/all_to_all | solution.py:324
  15.5 0.1 convert_element_type.31
  15.6 0.1 select_reduce_fusion.slot_ref
  15.7 7.6 %all-to-all-done.1.got_ref = f32[128,8,128]{2,1,0:T(8,128)S(1)} async-done(((f32[128,8,128]{2,1,0:T(8,128)}), f32[128,8,128]{2,1,0:T(8,128)S(1)}, u32[]{:S(2)}, u32[]{:S(2)}) %all-to-all-start.1) | async-done | bytes 524320 | tf_op jit(solution)/shard_map/all_to_all | solution.py:324
  23.3 16.4 %elements.1 = (f32[128,3,128]{2,1,0:T(4,128)}, f32[3,128,512]{2,1,0:T(8,128)S(1)}, f32[3,64,640]{2,1,0:T(8,128)S(1)}, f32[3,64,640]{2,1,0:T(8,128)S(1)}) custom-call(s32[128]{0:T(128)S(1)} %select_reduce_fusion.slot_ref, s32[128]{0:T(128)S(1)} %get-tuple-element.26.count_ref, f32[128,8,128]{2,1,0:T(8,128)S(1)} %all-to-all-done.1.got_ref, ...), custom_call_target="tpu_custom_call" | custom-call | flops 200000000 | bytes 4000000 | tf_op jit(solution)/shard_map/elements/pallas_call | solution.py:182
  39.7 3.0 %collective-permute-start.1 = (f32[3,64,640]{2,1,0:T(8,128)S(1)}, f32[3,64,640]{2,1,0:T(8,128)S(1)}, u32[]{:S(2)}, u32[]{:S(2)}) collective-permute-start(f32[3,64,640]{2,1,0:T(8,128)S(1)} %get-tuple-element.11.prev_ref), channel_id=1, source_target_pairs={{4,0},{8,4},{12,8},{16,12},{20,16},{24,20},{28,24},{5,1},{9,5},{13... | collective-permute-start | bytes 1474568 | tf_op jit(solution)/shard_map/ppermute | solution.py:303
  42.8 2.2 %collective-permute-start = (f32[3,64,640]{2,1,0:T(8,128)S(1)}, f32[3,64,640]{2,1,0:T(8,128)S(1)}, u32[]{:S(2)}, u32[]{:S(2)}) collective-permute-start(f32[3,64,640]{2,1,0:T(8,128)S(1)} %get-tuple-element.12.next_ref), channel_id=1, source_target_pairs={{0,4},{4,8},{8,12},{12,16},{16,20},{20,24},{24,28},{1,5},{5,9},{9,... | collective-permute-start | bytes 1474568 | tf_op jit(solution)/shard_map/ppermute | solution.py:303
  45.0 5.5 %all-to-all-start.2 = ((f32[128,3,128]{2,1,0:T(4,128)}), f32[128,3,128]{2,1,0:T(4,128)}, u32[]{:S(2)}, u32[]{:S(2)}) async-start(f32[128,3,128]{2,1,0:T(4,128)} %get-tuple-element.9), calls=%async_computation.2 | async-start | bytes 524288 | tf_op jit(solution)/shard_map/all_to_all | solution.py:331
  50.6 13.4 %collective-permute-done.1.from_next = f32[3,64,640]{2,1,0:T(8,128)S(1)} collective-permute-done((f32[3,64,640]{2,1,0:T(8,128)S(1)}, f32[3,64,640]{2,1,0:T(8,128)S(1)}, u32[]{:S(2)}, u32[]{:S(2)}) %collective-permute-start.1) | collective-permute-done | bytes 491552 | tf_op jit(solution)/shard_map/ppermute | solution.py:303
  64.0 1.3 %collective-permute-done.from_prev = f32[3,64,640]{2,1,0:T(8,128)S(1)} collective-permute-done((f32[3,64,640]{2,1,0:T(8,128)S(1)}, f32[3,64,640]{2,1,0:T(8,128)S(1)}, u32[]{:S(2)}, u32[]{:S(2)}) %collective-permute-start) | collective-permute-done | bytes 491552 | tf_op jit(solution)/shard_map/ppermute | solution.py:303
  65.2 1.0 %xpass.1 = (f32[3,2,4,16,512]{4,3,2,1,0:T(8,128)S(1)}, f32[3,2,16,128]{3,2,1,0:T(8,128)}, f32[3,2,16,128]{3,2,1,0:T(8,128)}) custom-call(f32[3,2,4,16,512]{4,3,2,1,0:T(8,128)S(1)} %bitcast.7, f32[3,64,640]{2,1,0:T(8,128)S(1)} %get-tuple-element.11.prev_ref, f32[3,64,640]{2,1,0:T(8,128)S(1)} %get-tuple-element.12.next_ref, ...), custom_call_target="tpu_custom_call" | custom-call | tf_op jit(solution)/shard_map/xpass/pallas_call | solution.py:290
  66.2 2.5 %collective-permute-start.2 = (f32[3,2,16,128]{3,2,1,0:T(8,128)}, f32[3,2,16,128]{3,2,1,0:T(8,128)S(1)}, u32[]{:S(2)}, u32[]{:S(2)}) collective-permute-start(f32[3,2,16,128]{3,2,1,0:T(8,128)} %get-tuple-element.14), channel_id=1, source_target_pairs={{1,0},{2,1},{3,2},{5,4},{6,5},{7,6},{9,8},{10,9},{11,10},{13,12},{... | collective-permute-start | bytes 147464 | tf_op jit(solution)/shard_map/ppermute | solution.py:303
  68.7 3.1 %collective-permute-start.3 = (f32[3,2,16,128]{3,2,1,0:T(8,128)}, f32[3,2,16,128]{3,2,1,0:T(8,128)S(1)}, u32[]{:S(2)}, u32[]{:S(2)}) collective-permute-start(f32[3,2,16,128]{3,2,1,0:T(8,128)} %get-tuple-element.15), channel_id=1, source_target_pairs={{0,1},{1,2},{2,3},{4,5},{5,6},{6,7},{8,9},{9,10},{10,11},{12,13},{... | collective-permute-start | bytes 147464 | tf_op jit(solution)/shard_map/ppermute | solution.py:303
  71.8 1.7 %gather_fusion.2 = f32[128,3,128]{2,1,0:T(4,128)S(1)} fusion(f32[128,3,128]{2,1,0:T(4,128)} %all-to-all-done.2, s32[1024]{0:T(1024)S(1)} %pad_clamp_fusion), kind=kCustom, calls=%fused_computation.2 | custom fusion | bytes 393728 | tf_op jit(solution)/shard_map/gather | solution.py:332
  73.5 0.7 copy.21
  74.2 7.1 %yzpass.1 = f32[3,2,4,16,512]{4,3,2,1,0:T(8,128)} custom-call(f32[3,2,4,16,512]{4,3,2,1,0:T(8,128)S(1)} %get-tuple-element.13.field_ref, f32[3,2,16,128]{3,2,1,0:T(8,128)S(1)} %collective-permute-done.2.far_lo_ref, f32[3,2,16,128]{3,2,1,0:T(8,128)S(1)} %collective-permute-done.3.far_hi_ref), custom_call_target="tpu_custom_call" | custom-call | tf_op jit(solution)/shard_map/yzpass/pallas_call | solution.py:290
  (19 shorter events, 0.1 us)
Async XLA Ops:
  0.6 0.9 %copy-start.4 = (s32[128]{0:T(128)S(1)}, s32[128]{0:T(128)}, u32[]{:S(2)}) copy-start(s32[128]{0:T(128)} %param.12) | copy-start | bytes 1540
  1.7 0.7 copy-start.5
  1.7 0.7 copy-start.6
  2.4 5.8 %copy-start.1 = (f32[128,3,128]{2,0,1:T(8,128)S(1)}, f32[128,3,128]{2,0,1:T(8,128)}, u32[]{:S(2)}) copy-start(f32[128,3,128]{2,0,1:T(8,128)} %param.8) | copy-start | bytes 589828
  4.3 7.4 %all-to-all-start = ((f32[4,1,32]{2,1,0:T(1,128)}), f32[4,1,32]{2,1,0:T(1,128)S(1)}, u32[]{:S(2)}, u32[]{:S(2)}) async-start(f32[4,1,32]{2,1,0:T(1,128)} %bitcast.2), calls=%async_computation | async-start | bytes 4096 | tf_op jit(solution)/shard_map/all_to_all | solution.py:325
  8.2 0.9 %copy-start.2 = (f32[128,3,128]{2,0,1:T(8,128)S(1)}, f32[128,3,128]{2,0,1:T(8,128)}, u32[]{:S(2)}) copy-start(f32[128,3,128]{2,0,1:T(8,128)} %param.9) | copy-start | bytes 589828
  9.1 0.9 %copy-start.3 = (f32[128,2,128]{2,1,0:T(2,128)S(1)}, f32[128,2,128]{2,1,0:T(2,128)}, u32[]{:S(2)}) copy-start(f32[128,2,128]{2,1,0:T(2,128)} %param.10) | copy-start | bytes 393220
  11.7 11.6 %copy-start = (bf16[3,2,4,16,512]{4,3,2,1,0:T(8,128)(2,1)S(1)}, bf16[3,2,4,16,512]{4,3,2,1,0:T(8,128)(2,1)}, u32[]{:S(2)}) copy-start(bf16[3,2,4,16,512]{4,3,2,1,0:T(8,128)(2,1)} %param.7) | copy-start | bytes 1179652
  11.7 11.6 %all-to-all-start.1 = ((f32[128,8,128]{2,1,0:T(8,128)}), f32[128,8,128]{2,1,0:T(8,128)S(1)}, u32[]{:S(2)}, u32[]{:S(2)}) async-start(f32[128,8,128]{2,1,0:T(8,128)} %gather_fusion.1), calls=%async_computation.1 | async-start | bytes 1048576 | tf_op jit(solution)/shard_map/all_to_all | solution.py:324
  39.7 24.2 %collective-permute-start.1 = (f32[3,64,640]{2,1,0:T(8,128)S(1)}, f32[3,64,640]{2,1,0:T(8,128)S(1)}, u32[]{:S(2)}, u32[]{:S(2)}) collective-permute-start(f32[3,64,640]{2,1,0:T(8,128)S(1)} %get-tuple-element.11.prev_ref), channel_id=1, source_target_pairs={{4,0},{8,4},{12,8},{16,12},{20,16},{24,20},{28,24},{5,1},{9,5},{13... | collective-permute-start | bytes 1474568 | tf_op jit(solution)/shard_map/ppermute | solution.py:303
  42.8 22.5 %collective-permute-start = (f32[3,64,640]{2,1,0:T(8,128)S(1)}, f32[3,64,640]{2,1,0:T(8,128)S(1)}, u32[]{:S(2)}, u32[]{:S(2)}) collective-permute-start(f32[3,64,640]{2,1,0:T(8,128)S(1)} %get-tuple-element.12.next_ref), channel_id=1, source_target_pairs={{0,4},{4,8},{8,12},{12,16},{16,20},{20,24},{24,28},{1,5},{5,9},{9,... | collective-permute-start | bytes 1474568 | tf_op jit(solution)/shard_map/ppermute | solution.py:303
  45.0 26.8 %all-to-all-start.2 = ((f32[128,3,128]{2,1,0:T(4,128)}), f32[128,3,128]{2,1,0:T(4,128)}, u32[]{:S(2)}, u32[]{:S(2)}) async-start(f32[128,3,128]{2,1,0:T(4,128)} %get-tuple-element.9), calls=%async_computation.2 | async-start | bytes 524288 | tf_op jit(solution)/shard_map/all_to_all | solution.py:331
  66.2 8.0 %collective-permute-start.2 = (f32[3,2,16,128]{3,2,1,0:T(8,128)}, f32[3,2,16,128]{3,2,1,0:T(8,128)S(1)}, u32[]{:S(2)}, u32[]{:S(2)}) collective-permute-start(f32[3,2,16,128]{3,2,1,0:T(8,128)} %get-tuple-element.14), channel_id=1, source_target_pairs={{1,0},{2,1},{3,2},{5,4},{6,5},{7,6},{9,8},{10,9},{11,10},{13,12},{... | collective-permute-start | bytes 147464 | tf_op jit(solution)/shard_map/ppermute | solution.py:303
  68.7 5.5 %collective-permute-start.3 = (f32[3,2,16,128]{3,2,1,0:T(8,128)}, f32[3,2,16,128]{3,2,1,0:T(8,128)S(1)}, u32[]{:S(2)}, u32[]{:S(2)}) collective-permute-start(f32[3,2,16,128]{3,2,1,0:T(8,128)} %get-tuple-element.15), channel_id=1, source_target_pairs={{0,1},{1,2},{2,3},{4,5},{5,6},{6,7},{8,9},{9,10},{10,11},{12,13},{... | collective-permute-start | bytes 147464 | tf_op jit(solution)/shard_map/ppermute | solution.py:303

commit v2 on v1

v2 whole, which is shorter than its diff:
```python
import functools

import jax
import jax.numpy as jnp
from jax import lax
from jax.experimental import pallas as pl
from jax.experimental.pallas import tpu as pltpu
from jax.sharding import PartitionSpec as P

GLL = (
    -1.0,
    -0.8717401485096066,
    -0.5917001814331423,
    -0.2092992179024789,
    0.2092992179024789,
    0.5917001814331423,
    0.8717401485096066,
    1.0,
)
SHARPNESS = 8.0
VMEM = pltpu.VMEM
SMEM = pltpu.SMEM
ROWS = 24


def lane_iota(shape):
    return lax.broadcasted_iota(jnp.int32, shape, len(shape) - 1)


def node_consts():
    row = lax.broadcasted_iota(jnp.int32, (8, 128), 0)

    def pick(values):
        out = jnp.full((8, 128), values[7], jnp.float32)
        for i in range(7):
            out = jnp.where(row == i, jnp.float32(values[i]), out)
        return out

    others = [pick([[GLL[m] for m in range(8) if m != i][n] for i in range(8)]) for n in range(7)]
    scales = []
    for i in range(8):
        product = 1.0
        for m in range(8):
            if m != i:
                product *= GLL[i] - GLL[m]
        scales.append(1.0 / product)
    return pick(GLL), others, pick(scales)


def lagrange(x, others, scale):
    diffs = [x - o for o in others]
    left = (diffs[0] * diffs[1]) * (diffs[2] * diffs[3])
    right = (diffs[4] * diffs[5]) * (diffs[6] * scale)
    return left * right


def gauss(x, nodes):
    gap = nodes - x
    return jnp.exp(-SHARPNESS * gap * gap)


def split(x):
    high = x.astype(jnp.bfloat16)
    low = (x - high.astype(jnp.float32)).astype(jnp.bfloat16)
    return high, low


def planes(a, b):
    return jnp.concatenate([a[j : j + 1] * b for j in range(8)], axis=0)


def spread_nodes(vel_ref, vs_ref, elems):
    low = lane_iota((elems, 128)) < 64
    for c in range(3):
        for q in range(4):
            x = vel_ref[c, :, q * 128 : (q + 1) * 128].astype(jnp.float32)
            turned = pltpu.roll(x, 64, 1)
            vs_ref[pl.ds(c * 8 + 2 * q, elems, stride=ROWS), :] = jnp.where(low, x, turned)
            vs_ref[pl.ds(c * 8 + 2 * q + 1, elems, stride=ROWS), :] = jnp.where(low, turned, x)


def st_planes(s, t, nodes):
    high, low = split(planes(gauss(s, nodes), gauss(t, nodes)))
    gathered = jnp.concatenate([high, low], axis=0)
    return jnp.concatenate([gathered, gathered], axis=1)


def project(left, gathered):
    high, low = split(left)
    return lax.dot_general(
        jnp.concatenate([high, low], axis=1),
        gathered,
        (((1,), (1,)), ((), ())),
        preferred_element_type=jnp.float32,
    )


def element(block, count, field, consts, inner_minus, inner_plus):
    nodes, others, scale = consts
    r, s, t = (jnp.broadcast_to(block[d : d + 1], (8, 128)) for d in range(3))
    basis_r = lagrange(r, others, scale)
    basis_st = planes(lagrange(s, others, scale), lagrange(t, others, scale))
    high, low = split(basis_st)
    partial = jnp.dot(
        field.astype(jnp.bfloat16),
        jnp.concatenate([high, low], axis=0),
        preferred_element_type=jnp.float32,
    )
    rel = []
    for c in range(3):
        fluid = jnp.sum(partial[c * 8 : c * 8 + 8] * basis_r, axis=0, keepdims=True)
        rel.append(fluid - block[3 + c : 4 + c])
    speed = jnp.sqrt(rel[0] * rel[0] + rel[1] * rel[1] + rel[2] * rel[2])
    power = jnp.exp(0.687 * jnp.log(block[7:8] * speed))
    factor = block[6:7] * (1.0 + 0.15 * power)
    factor = jnp.where(lane_iota((1, 128)) < count, factor, 0.0)
    drag = [factor * w for w in rel]
    whole = jnp.concatenate(drag, axis=0)
    minus = gauss(r + 2.0, nodes)
    plus = gauss(r - 2.0, nodes)
    weights = [gauss(r, nodes)]
    if inner_minus:
        weights.append(minus)
    if inner_plus:
        weights.append(plus)
    rows = [(-d) * w for w in weights for d in drag]
    blank = jnp.zeros((5, 128), jnp.float32)
    if not inner_minus:
        rows.append(jnp.concatenate([-whole * minus[7:8], blank], axis=0))
    if not inner_plus:
        rows.append(jnp.concatenate([-whole * plus[0:1], blank], axis=0))
    out = project(jnp.concatenate(rows, axis=0), st_planes(s, t, nodes))
    parts, at = {}, ROWS
    parts["own"] = out[0:ROWS]
    for name, inner in (("minus", inner_minus), ("plus", inner_plus)):
        if inner:
            parts[name] = out[at : at + ROWS]
            at += ROWS
    for name, inner in (("minus", inner_minus), ("plus", inner_plus)):
        if not inner:
            parts[name] = out[at : at + 8]
            at += 8
    return whole, parts


def main_kernel(
    shape, chunks, n_gx, n_gy,
    slot_ref, count_ref, elem_ref, got_ref, vel_ref,
    field_ref, far_lo_ref, far_hi_ref, ret_ref,
    vs_ref, ts_ref, fs_ref, drag_ref, pos_ref, gpos_ref, gdrag_ref,
    face_ref, gface_ref, lo_ref, hi_ref, back_ref,
    pos_sem, drag_sem, face_sem, y_sem, back_sem,
):
    exd, eyd, ez = shape
    elems = exd * eyd * ez
    columns = eyd * ez
    share = elems // n_gy
    group = 4
    turns = columns // group
    per = turns // chunks
    wide = columns // chunks
    half = columns // 2
    gx = lax.axis_index("gx")
    gy = lax.axis_index("gy")
    has = (gx > 0, gx < n_gx - 1)
    mesh_id = pl.DeviceIdType.MESH

    def to_side(side, src, dst, sems, *at):
        return pltpu.make_async_remote_copy(
            src_ref=src, dst_ref=dst,
            send_sem=sems.at[(0, side) + at], recv_sem=sems.at[(1, 1 - side) + at],
            device_id={"gx": gx - 1 if side == 0 else gx + 1}, device_id_type=mesh_id,
        )

    def from_side(side, src, dst, sems, *at):
        return pltpu.make_async_remote_copy(
            src_ref=src, dst_ref=dst,
            send_sem=sems.at[(0, side) + at], recv_sem=sems.at[(1, side) + at],
            device_id={"gx": gx - 1 if side == 0 else gx + 1}, device_id_type=mesh_id,
        )

    barrier = pltpu.get_barrier_semaphore()
    for side in range(2):
        @pl.when(has[side])
        def _():
            pl.semaphore_signal(
                barrier, inc=1, device_id={"gx": gx - 1 if side == 0 else gx + 1}, device_id_type=mesh_id
            )
    for off in range(1, n_gy):
        pl.semaphore_signal(
            barrier, inc=1, device_id={"gy": lax.rem(gy + off, n_gy)}, device_id_type=mesh_id
        )

    base = (0, elems - columns)

    def stage(col, carry):
        for side in range(2):
            pos_ref[side, col] = got_ref[slot_ref[base[side] + col], 0:3]
        return carry

    lax.fori_loop(0, columns, stage, 0, unroll=4)
    pl.semaphore_wait(
        barrier, n_gy - 1 + (gx > 0).astype(jnp.int32) + (gx < n_gx - 1).astype(jnp.int32)
    )
    for side in range(2):
        @pl.when(has[side])
        def _():
            to_side(side, pos_ref.at[side], gpos_ref.at[1 - side], pos_sem).start()

    spread_nodes(vel_ref, vs_ref, elems)
    consts = node_consts()
    nodes = consts[0]

    def drag_copy(make, side, chunk):
        start = base[side] + chunk * wide
        return make(
            side, drag_ref.at[pl.ds(start, wide)], gdrag_ref.at[1 - side, pl.ds(chunk * wide, wide)], drag_sem, chunk
        )

    def turn(index, carry):
        for g in range(group):
            col = index * group + g
            parts = []
            for x in range(exd):
                e = x * columns + col
                slot = slot_ref[e]
                drag, part = element(
                    got_ref[slot],
                    count_ref[slot],
                    vs_ref[pl.ds(pl.multiple_of(e * ROWS, 8), ROWS), :],
                    consts,
                    x > 0,
                    x + 1 < exd,
                )
                drag_ref[e] = drag
                parts.append(part)
            for x in range(exd):
                e = x * columns + col
                own = parts[x]["own"]
                if x + 1 < exd:
                    own = own + parts[x + 1]["minus"]
                if x > 0:
                    own = own + parts[x - 1]["plus"]
                ts_ref[pl.ds(pl.multiple_of(e * ROWS, 8), ROWS), :] = own
            start = pl.multiple_of(col * 8, 8)
            fs_ref[0, pl.ds(start, 8), :] = parts[0]["minus"]
            fs_ref[1, pl.ds(start, 8), :] = parts[exd - 1]["plus"]
        for side in range(2):
            @pl.when((lax.rem(index, per) == per - 1) & has[side])
            def _():
                drag_copy(to_side, side, lax.div(index, per)).start()
        return carry

    lax.fori_loop(0, turns, turn, 0)

    def doubled(x):
        return x + pltpu.roll(x, 64, 1)

    low_h = lane_iota((half, 128)) < 64
    for side in range(2):
        node = 0 if side == 0 else 7
        for c in range(3):
            one = doubled(ts_ref[pl.ds(base[side] * ROWS + c * 8 + node, half, stride=ROWS), :])
            two = doubled(ts_ref[pl.ds((base[side] + half) * ROWS + c * 8 + node, half, stride=ROWS), :])
            face_ref[side, c] = jnp.where(low_h, one, two)
        @pl.when(has[side])
        def _():
            to_side(side, face_ref.at[side], gface_ref.at[1 - side], face_sem).start()

    def fill(k, carry):
        back_ref[k] = drag_ref[elem_ref[k]]
        return carry

    lax.fori_loop(0, elems, fill, 0, unroll=4)

    def back_copy(off):
        peer = lax.rem(gy + off, n_gy)
        return pltpu.make_async_remote_copy(
            src_ref=back_ref.at[pl.ds(peer * share, share)], dst_ref=ret_ref.at[pl.ds(gy * share, share)],
            send_sem=back_sem.at[0, off - 1], recv_sem=back_sem.at[1, off - 1],
            device_id={"gy": peer}, device_id_type=mesh_id,
        )

    for off in range(1, n_gy):
        back_copy(off).start()

    def keep(k, carry):
        ret_ref[gy * share + k] = back_ref[gy * share + k]
        return carry

    lax.fori_loop(0, share, keep, 0, unroll=4)

    for side in range(2):
        @pl.when(has[side])
        def _():
            from_side(side, pos_ref.at[side], gpos_ref.at[side], pos_sem).wait()

        def ghost(index, carry):
            @pl.when(lax.rem(index, per) == 0)
            def _():
                chunk = lax.div(index, per)
                from_side(
                    side, drag_ref.at[pl.ds(base[side] + chunk * wide, wide)],
                    gdrag_ref.at[side, pl.ds(chunk * wide, wide)], drag_sem, chunk,
                ).wait()

            for g in range(group):
                col = index * group + g
                place = gpos_ref[side, col]
                force = gdrag_ref[side, col]
                r, s, t = (jnp.broadcast_to(place[d : d + 1], (8, 128)) for d in range(3))
                weight = gauss(r + (-2.0 if side == 0 else 2.0), nodes)
                rows = [(-force[c : c + 1]) * weight for c in range(3)]
                add = project(jnp.concatenate(rows, axis=0), st_planes(s, t, nodes))
                spot = pl.ds(pl.multiple_of((base[side] + col) * ROWS, 8), ROWS)
                ts_ref[spot, :] = ts_ref[spot, :] + add
            return carry

        @pl.when(has[side])
        def _():
            lax.fori_loop(0, turns, ghost, 0)

    for side in range(2):
        @pl.when(has[side])
        def _():
            from_side(side, face_ref.at[side], gface_ref.at[side], face_sem).wait()

    low = lane_iota((ez, 128)) < 64
    spot64 = lane_iota((ez, 128)) % 64

    def lanes(c, x, y, q):
        start = ((x * eyd + y) * ez) * ROWS + c * 8 + 2 * q
        even = ts_ref[pl.ds(start, ez, stride=ROWS), :]
        odd = ts_ref[pl.ds(start + 1, ez, stride=ROWS), :]
        return jnp.where(low, even, odd) + pltpu.roll(jnp.where(low, odd, even), 64, 1)

    def far(side, c, y):
        col = y * ez
        upper = col >= half
        row = col - half if upper else col
        came = gface_ref[side, c, row : row + ez, :]
        turned = pltpu.roll(came, 64, 1)
        came = jnp.where(low, turned, came) if upper else jnp.where(low, came, turned)
        mine = doubled(fs_ref[side, pl.ds(col * 8 + c, ez, stride=8), :])
        return jnp.where(has[side], came + mine, 0.0)

    for y in (0, eyd - 1) + tuple(range(1, eyd - 1)):
        for c in range(3):
            grid = [[lanes(c, x, y, q) for q in range(4)] for x in range(exd)]
            for x in range(exd):
                above = pltpu.roll(grid[x + 1][0], 64, 1) if x + 1 < exd else far(1, c, y)
                below = pltpu.roll(grid[x - 1][3], 64, 1) if x > 0 else far(0, c, y)
                done = list(grid[x])
                done[3] = done[3] + jnp.where(low, 0.0, above)
                done[0] = done[0] + jnp.where(low, below, 0.0)
                for q in range(4):
                    field_ref[c, x, y, :, q * 128 : (q + 1) * 128] = done[q]
                if y == 0:
                    face = jnp.where(spot64 < 8, done[0], 0.0)
                    for q in range(1, 4):
                        face = face + pltpu.roll(jnp.where(spot64 < 8, done[q], 0.0), 8 * q, 1)
                    lo_ref[c, x] = face
                if y == eyd - 1:
                    face = jnp.where(spot64 >= 56, done[0], 0.0)
                    for q in range(1, 4):
                        face = face + pltpu.roll(jnp.where(spot64 >= 56, done[q], 0.0), 128 - 8 * q, 1)
                    hi_ref[c, x] = face
        if y == eyd - 1:
            lo_copy = pltpu.make_async_remote_copy(
                src_ref=lo_ref, dst_ref=far_lo_ref, send_sem=y_sem.at[0, 0], recv_sem=y_sem.at[1, 0],
                device_id={"gy": gy - 1}, device_id_type=mesh_id,
            )
            hi_copy = pltpu.make_async_remote_copy(
                src_ref=hi_ref, dst_ref=far_hi_ref, send_sem=y_sem.at[0, 1], recv_sem=y_sem.at[1, 1],
                device_id={"gy": gy + 1}, device_id_type=mesh_id,
            )
            @pl.when(gy > 0)
            def _():
                lo_copy.start()
            @pl.when(gy < n_gy - 1)
            def _():
                hi_copy.start()

    @pl.when(gy > 0)
    def _():
        lo_copy.wait_send()
        hi_copy.wait_recv()
    @pl.when(gy < n_gy - 1)
    def _():
        hi_copy.wait_send()
        lo_copy.wait_recv()
    for off in range(1, n_gy):
        back_copy(off).wait()


def run_main(slot, count, elem_of, got, velocity, shape):
    exd, eyd, ez = shape
    elems = exd * eyd * ez
    columns = eyd * ez
    n_gx, n_gy = lax.axis_size("gx"), lax.axis_size("gy")
    chunks = 4
    f32 = jnp.float32
    dma = pltpu.SemaphoreType.DMA
    face = (3, exd, ez, 128)
    return pl.pallas_call(
        functools.partial(main_kernel, shape, chunks, n_gx, n_gy),
        out_shape=(
            jax.ShapeDtypeStruct((3, exd, eyd, ez, 512), f32),
            jax.ShapeDtypeStruct(face, f32),
            jax.ShapeDtypeStruct(face, f32),
            jax.ShapeDtypeStruct((elems, 3, 128), f32),
        ),
        in_specs=[pl.BlockSpec(memory_space=SMEM)] * 3 + [pl.BlockSpec(memory_space=VMEM)] * 2,
        out_specs=[pl.BlockSpec(memory_space=VMEM)] * 4,
        scratch_shapes=[
            pltpu.VMEM((elems * ROWS, 128), f32),
            pltpu.VMEM((elems * ROWS, 128), f32),
            pltpu.VMEM((2, columns * 8, 128), f32),
            pltpu.VMEM((elems, 3, 128), f32),
            pltpu.VMEM((2, columns, 3, 128), f32),
            pltpu.VMEM((2, columns, 3, 128), f32),
            pltpu.VMEM((2, columns, 3, 128), f32),
            pltpu.VMEM((2, 3, columns // 2, 128), f32),
            pltpu.VMEM((2, 3, columns // 2, 128), f32),
            pltpu.VMEM(face, f32),
            pltpu.VMEM(face, f32),
            pltpu.VMEM((elems, 3, 128), f32),
            dma((2, 2)),
            dma((2, 2, chunks)),
            dma((2, 2)),
            dma((2, 2)),
            dma((2, n_gy - 1)),
        ],
        compiler_params=pltpu.CompilerParams(
            vmem_limit_bytes=48 * 1024 * 1024, collective_id=0, has_side_effects=True
        ),
        cost_estimate=pl.CostEstimate(flops=200_000_000, bytes_accessed=4_000_000, transcendentals=700_000),
        name="elements",
    )(slot, count, elem_of, got, velocity)


def yz_pass(position_ref, field_ref, far_lo_ref, far_hi_ref, ret_ref, out_ref, drag_ref, buf_ref, sem):
    _, exd, eyd, ez, _ = field_ref.shape
    at = lax.axis_index("gy")
    first = at > 0
    last = at < lax.axis_size("gy") - 1
    place = lane_iota((ez, 128)) % 64
    k = lane_iota((ez, 128)) % 8
    row = lax.broadcasted_iota(jnp.int32, (ez, 128), 0)
    up = (k == 7) & (row < ez - 1)
    down = (k == 0) & (row > 0)
    copies = []
    for c in range(3):
        for x in range(exd):
            far_lo = jnp.where(last, far_lo_ref[c, x], 0.0)
            far_hi = jnp.where(first, far_hi_ref[c, x], 0.0)
            for q in range(4):
                spot = slice(q * 128, (q + 1) * 128)
                cells = [field_ref[c, x, y, :, spot] for y in range(eyd)]
                for y in range(eyd):
                    if y + 1 < eyd:
                        above = pltpu.roll(cells[y + 1], 56, 1)
                    else:
                        above = pltpu.roll(far_lo, (56 - 8 * q) % 128, 1)
                    if y > 0:
                        below = pltpu.roll(cells[y - 1], 72, 1)
                    else:
                        below = pltpu.roll(far_hi, (72 + 8 * q) % 128, 1)
                    v = cells[y] + jnp.where(place >= 56, above, 0.0) + jnp.where(place < 8, below, 0.0)
                    nxt = pltpu.roll(pltpu.roll(v, ez - 1, 0), 7, 1)
                    prv = pltpu.roll(pltpu.roll(v, 1, 0), 121, 1)
                    buf_ref[c, x, y, :, spot] = v + jnp.where(up, nxt, 0.0) + jnp.where(down, prv, 0.0)


            copies.append(pltpu.make_async_copy(buf_ref.at[c, x], out_ref.at[c, x], sem.at[c, x]))
            copies[-1].start()

    def pick(b, carry):
        drag_ref[b] = ret_ref[position_ref[b]]
        return carry

    lax.fori_loop(0, ret_ref.shape[0], pick, 0, unroll=4)
    for copy in copies:
        copy.wait()


def run_yz(position, field, far_lo, far_hi, ret):
    f32 = jnp.float32
    return pl.pallas_call(
        yz_pass,
        out_shape=(jax.ShapeDtypeStruct(field.shape, f32), jax.ShapeDtypeStruct(ret.shape, f32)),
        in_specs=[pl.BlockSpec(memory_space=SMEM)] + [pl.BlockSpec(memory_space=VMEM)] * 4,
        out_specs=[pl.BlockSpec(memory_space=pl.ANY), pl.BlockSpec(memory_space=VMEM)],
        scratch_shapes=[pltpu.VMEM(field.shape, f32), pltpu.SemaphoreType.DMA(field.shape[:2])],
        compiler_params=pltpu.CompilerParams(vmem_limit_bytes=32 * 1024 * 1024),
        name="yzpass",
    )(position, field, far_lo, far_hi, ret)


def inverse_of(position):
    n = position.shape[0]
    ladder = jnp.arange(n, dtype=jnp.int32)
    return jnp.sum(jnp.where(position[None, :] == ladder[:, None], ladder[None, :], 0), axis=1)


def body(velocity, part_pos, part_vel, part_coef, counts, dest, elem):
    _, exd, eyd, ez, nodes = velocity.shape
    elems = exd * eyd * ez
    devices = lax.axis_size("gy")
    share = elems // devices
    f32 = jnp.float32
    ladder = jnp.arange(elems, dtype=jnp.int32)
    earlier = (dest[None, :] == dest[:, None]) & (ladder[None, :] < ladder[:, None])
    position = dest * share + jnp.sum(earlier.astype(jnp.int32), axis=1)
    sorting = inverse_of(position)
    packed = jnp.concatenate([part_pos, part_vel, part_coef], axis=1)[sorting]
    labels = (elem * 256 + counts)[sorting].astype(f32)
    got = lax.all_to_all(packed, "gy", split_axis=0, concat_axis=0, tiled=True)
    got_labels = lax.all_to_all(labels.reshape(devices, share), "gy", split_axis=0, concat_axis=0, tiled=True)
    got_labels = got_labels.reshape(elems).astype(jnp.int32)
    slot = inverse_of(got_labels // 256)
    field, far_lo, far_hi, ret = run_main(
        slot, got_labels % 256, got_labels // 256, got,
        velocity.reshape(3, elems, nodes), (exd, eyd, ez),
    )
    source, drag_out = run_yz(position, field, far_lo, far_hi, ret)
    return (drag_out, source)


def solution(mesh):
    in_specs = (
        P(None, "gx", "gy", None, None),
        P(("gx", "gy"), None, None),
        P(("gx", "gy"), None, None),
        P(("gx", "gy"), None, None),
        P(("gx", "gy")),
        P(("gx", "gy")),
        P(("gx", "gy")),
    )
    out_specs = (P(("gx", "gy"), None, None), P(None, "gx", "gy", None, None))
    return jax.shard_map(body, mesh=mesh, in_specs=in_specs, out_specs=out_specs, check_vma=False)
```

time: 82.8 us -> 60.9 us (0.74); the launches traced: 81.3 us -> 60.7 us
  starting transfers between devices: 23.9 us -> 7.58 us
  waiting for transfers between devices: 22.3 us -> 7.62 us
  Pallas kernels: 24.5 us -> 36.6 us
  local copies, waits for them, and re-layouts: 8.41 us -> 6.7 us
    ppermute x4 -> x0, waiting for transfers between devices: 14.7 us -> none  [shifted(): return lax.ppermute(shard, axis, pairs)]
    pallas_call x3 -> x2, Pallas kernels: 24.5 us -> 36.6 us  [the longest x1 29.1 us: run_main(): pl.pallas_call(functools.partial(main_kernel, shape, chunks, n_gx, n_gy),...]
    ppermute x4 -> x0, starting transfers between devices: 10.8 us -> none  [shifted(): return lax.ppermute(shard, axis, pairs)]
    all_to_all x1 -> x0, starting transfers between devices: 5.54 us -> none  [body(): lax.all_to_all(drag_slots, 'gy', split_axis=0, concat_axis=0, tiled=True)]
    gather x1 -> x0, local copies, waits for them, and re-layouts: 1.71 us -> none  [body(): drag_out = returned[position]]
  transfers between devices with their start and end apart: 7 -> 2, of which waited for: 3 -> 1; matrix products, arithmetic and copies ran while one was open for 6% -> 4% of each run, Pallas kernels for 1% -> 0%
where the time goes in v2:
time: 60.9 us; the launch traced here: 60.7 us
  Pallas kernels  36.6 us (60%)
  waiting for transfers between devices  7.62 us (13%)
  starting transfers between devices  7.58 us (12%)
  local copies, waits for them, and re-layouts  6.7 us (11%)
  other arithmetic  1.36 us (2%)
  between operations  0.75 us (1%)
    pallas_call x1, Pallas kernels, run_main(): pl.pallas_call(functools.partial(main_kernel, shape, chunks, n_gx, n_gy),...  29.1 us
    all_to_all x1, waiting for transfers between devices, body(): got = lax.all_to_all(packed, 'gy', split_axis=0, concat_axis=0, tiled=True)  7.62 us
    pallas_call x1, Pallas kernels, run_yz(): pl.pallas_call(yz_pass, out_shape=(jax.ShapeDtypeStruct(field.shape, f32)...  7.5 us
    all_to_all x1, starting transfers between devices, body(): lax.all_to_all(labels.reshape(devices, share), 'gy', split_axis=0, concat...  3.86 us
    all_to_all x1, starting transfers between devices, body(): got = lax.all_to_all(packed, 'gy', split_axis=0, concat_axis=0, tiled=True)  3.71 us
    unnamed x17, local copies, waits for them, and re-layouts  3.17 us
    gather x1, local copies, waits for them, and re-layouts, body(): packed = jnp.concatenate([part_pos, part_vel, part_coef], axis=1)[sorting]  1.55 us
    gather x1, local copies, waits for them, and re-layouts, body(): labels = (elem * 256 + counts)[sorting].astype(f32)  1.22 us
  transfers between devices with their start and end apart: 2, of which 1 were waited for; matrix products, arithmetic and copies ran while one was open for 4% of the time, Pallas kernels for 0%

profile of v2, /device:TPU:17, one launch (start us, length us, event | category | flops | bytes accessed | tf_op | source)
XLA Modules:
  0.0 60.7 jit_solution(17686180291866394153)
XLA Ops:
  0.6 0.0 copy-start.4
  0.6 0.9 %convert_reduce_fusion = s32[128]{0:T(128)S(1)} fusion(s32[128]{0:T(128)} %param.12), kind=kLoop, calls=%fused_computation.7 | loop fusion | flops 81792 | bytes 1024 | tf_op jit(solution)/shard_map/reduce_sum | solution.py:514
  1.6 0.0 copy-done.4
  1.6 0.1 select_reduce_fusion.1
  1.7 0.0 copy-start.5
  1.7 0.0 copy-start.6
  1.7 0.6 %copy-done.5 = s32[128]{0:T(128)S(1)} copy-done((s32[128]{0:T(128)S(1)}, s32[128]{0:T(128)}, u32[]{:S(2)}) %copy-start.5) | copy-done | bytes 536
  2.4 0.0 copy-done.6
  2.4 0.0 copy-start.1
  2.4 1.2 %gather_fusion = s32[128]{0:T(128)S(1)} fusion(s32[128]{0:T(128)S(1)} %multiply_add_fusion, s32[1024]{0:T(1024)S(1)} %pad_clamp_fusion), kind=kCustom, calls=%fused_computation | custom fusion | bytes 1536 | tf_op jit(solution)/shard_map/gather | solution.py:517
  3.6 0.7 %convert_element_type.29 = f32[4,1,32]{2,0,1:T(4,128)} reshape(f32[128]{0:T(128)S(1)} %convert_element_type.28) | data formatting | bytes 1024 | tf_op jit(solution)/shard_map/convert_element_type | solution.py:517
  4.3 3.9 %all-to-all-start = ((f32[4,1,32]{2,1,0:T(1,128)}), f32[4,1,32]{2,1,0:T(1,128)S(1)}, u32[]{:S(2)}, u32[]{:S(2)}) async-start(f32[4,1,32]{2,1,0:T(1,128)} %bitcast.2), calls=%async_computation | async-start | bytes 4096 | tf_op jit(solution)/shard_map/all_to_all | solution.py:519
  8.2 0.0 copy-done.1
  8.2 0.0 copy-start.2
  8.2 0.1 copy.19
  8.3 0.8 %copy-done.2 = f32[128,3,128]{2,0,1:T(8,128)S(1)} copy-done((f32[128,3,128]{2,0,1:T(8,128)S(1)}, f32[128,3,128]{2,0,1:T(8,128)}, u32[]{:S(2)}) %copy-start.2) | copy-done | bytes 196632
  9.1 0.0 copy-start.3
  9.1 0.1 copy.20
  9.2 0.8 %copy-done.3 = f32[128,2,128]{2,1,0:T(2,128)S(1)} copy-done((f32[128,2,128]{2,1,0:T(2,128)S(1)}, f32[128,2,128]{2,1,0:T(2,128)}, u32[]{:S(2)}) %copy-start.3) | copy-done | bytes 131096
  10.0 0.2 pad_maximum_fusion
  10.2 1.6 %gather_fusion.1 = f32[128,8,128]{2,1,0:T(8,128)} fusion(f32[128,8,128]{2,1,0:T(8,128)S(1)} %pad_maximum_fusion, s32[1024]{0:T(1024)S(1)} %pad_clamp_fusion), kind=kCustom, calls=%fused_computation.1 | custom fusion | bytes 1049088 | tf_op jit(solution)/shard_map/gather | solution.py:516
  11.7 0.0 copy-start
  11.7 0.0 all-to-all-done
  11.7 3.7 %all-to-all-start.1 = ((f32[128,8,128]{2,1,0:T(8,128)}), f32[128,8,128]{2,1,0:T(8,128)S(1)}, u32[]{:S(2)}, u32[]{:S(2)}) async-start(f32[128,8,128]{2,1,0:T(8,128)} %gather_fusion.1), calls=%async_computation.1 | async-start | bytes 1048576 | tf_op jit(solution)/shard_map/all_to_all | solution.py:518
  15.5 0.1 convert_element_type.31
  15.6 0.1 select_reduce_fusion.slot_ref
  15.7 7.6 %all-to-all-done.1.got_ref = f32[128,8,128]{2,1,0:T(8,128)S(1)} async-done(((f32[128,8,128]{2,1,0:T(8,128)}), f32[128,8,128]{2,1,0:T(8,128)S(1)}, u32[]{:S(2)}, u32[]{:S(2)}) %all-to-all-start.1) | async-done | bytes 524320 | tf_op jit(solution)/shard_map/all_to_all | solution.py:518
  23.3 0.0 copy-done
  23.3 29.1 %elements.1 = (f32[3,2,4,16,512]{4,3,2,1,0:T(8,128)S(1)}, f32[3,2,16,128]{3,2,1,0:T(8,128)S(1)}, f32[3,2,16,128]{3,2,1,0:T(8,128)S(1)}, f32[128,3,128]{2,1,0:T(4,128)S(1)}) custom-call(s32[128]{0:T(128)S(1)} %select_reduce_fusion.slot_ref, s32[128]{0:T(128)S(1)} %get-tuple-element.22.count_ref, s32[128]{0:T(128)S(1)} %get-tuple-element.23.elem_ref, ...), custom_call_target="tpu_custom_call" | custom-call | flops 200000000 | bytes 4000000 | tf_op jit(solution)/shard_map/elements/pallas_call | solution.py:405
  52.5 7.5 %yzpass.1 = (f32[3,2,4,16,512]{4,3,2,1,0:T(8,128)}, f32[128,3,128]{2,1,0:T(4,128)S(1)}) custom-call(s32[128]{0:T(128)S(1)} %multiply_add_fusion.1.position_ref, f32[3,2,4,16,512]{4,3,2,1,0:T(8,128)S(1)} %get-tuple-element.8.field_ref, f32[3,2,16,128]{3,2,1,0:T(8,128)S(1)} %get-tuple-element.9.far_lo_ref, f32[3,2,16,128]{3,2,1,0:T(8,128)S(1)} %get-tuple-element.10.far_hi_ref, ...), custom_call_target="tpu_custom_call" | custom-call | tf_op jit(solution)/shard_map/yzpass/pallas_call | solution.py:489
  60.0 0.7 %copy.21 = f32[128,3,128]{2,0,1:T(8,128)} copy(f32[128,3,128]{2,1,0:T(4,128)S(1)} %get-tuple-element.20) | data formatting | bytes 393216
  (7 shorter events, 0.1 us)
Async XLA Ops:
  0.6 0.9 %copy-start.4 = (s32[128]{0:T(128)S(1)}, s32[128]{0:T(128)}, u32[]{:S(2)}) copy-start(s32[128]{0:T(128)} %param.12) | copy-start | bytes 1540
  1.7 0.7 %copy-start.5 = (s32[128]{0:T(128)S(1)}, s32[128]{0:T(128)}, u32[]{:S(2)}) copy-start(s32[128]{0:T(128)} %param.11) | copy-start | bytes 1540
  1.7 0.7 %copy-start.6 = (s32[128]{0:T(128)S(1)}, s32[128]{0:T(128)}, u32[]{:S(2)}) copy-start(s32[128]{0:T(128)} %param.13) | copy-start | bytes 1540
  2.4 5.8 %copy-start.1 = (f32[128,3,128]{2,0,1:T(8,128)S(1)}, f32[128,3,128]{2,0,1:T(8,128)}, u32[]{:S(2)}) copy-start(f32[128,3,128]{2,0,1:T(8,128)} %param.8) | copy-start | bytes 589828
  4.3 7.4 %all-to-all-start = ((f32[4,1,32]{2,1,0:T(1,128)}), f32[4,1,32]{2,1,0:T(1,128)S(1)}, u32[]{:S(2)}, u32[]{:S(2)}) async-start(f32[4,1,32]{2,1,0:T(1,128)} %bitcast.2), calls=%async_computation | async-start | bytes 4096 | tf_op jit(solution)/shard_map/all_to_all | solution.py:519
  8.2 0.9 %copy-start.2 = (f32[128,3,128]{2,0,1:T(8,128)S(1)}, f32[128,3,128]{2,0,1:T(8,128)}, u32[]{:S(2)}) copy-start(f32[128,3,128]{2,0,1:T(8,128)} %param.9) | copy-start | bytes 589828
  9.1 0.9 %copy-start.3 = (f32[128,2,128]{2,1,0:T(2,128)S(1)}, f32[128,2,128]{2,1,0:T(2,128)}, u32[]{:S(2)}) copy-start(f32[128,2,128]{2,1,0:T(2,128)} %param.10) | copy-start | bytes 393220
  11.7 11.6 %copy-start = (bf16[3,2,4,16,512]{4,3,2,1,0:T(8,128)(2,1)S(1)}, bf16[3,2,4,16,512]{4,3,2,1,0:T(8,128)(2,1)}, u32[]{:S(2)}) copy-start(bf16[3,2,4,16,512]{4,3,2,1,0:T(8,128)(2,1)} %param.7) | copy-start | bytes 1179652
  11.7 11.6 %all-to-all-start.1 = ((f32[128,8,128]{2,1,0:T(8,128)}), f32[128,8,128]{2,1,0:T(8,128)S(1)}, u32[]{:S(2)}, u32[]{:S(2)}) async-start(f32[128,8,128]{2,1,0:T(8,128)} %gather_fusion.1), calls=%async_computation.1 | async-start | bytes 1048576 | tf_op jit(solution)/shard_map/all_to_all | solution.py:518

commit v3 on v2

--- a/solution.py
+++ b/solution.py
@@ -193,12 +193,14 @@
 
     base = (0, elems - columns)
 
-    def stage(col, carry):
-        for side in range(2):
-            pos_ref[side, col] = got_ref[slot_ref[base[side] + col], 0:3]
+    def stage(index, carry):
+        spots = [(side, index * 4 + u) for side in range(2) for u in range(4)]
+        held = [got_ref[slot_ref[base[side] + col], 0:3] for side, col in spots]
+        for (side, col), value in zip(spots, held):
+            pos_ref[side, col] = value
         return carry
 
-    lax.fori_loop(0, columns, stage, 0, unroll=4)
+    lax.fori_loop(0, columns // 4, stage, 0)
     pl.semaphore_wait(
         barrier, n_gy - 1 + (gx > 0).astype(jnp.int32) + (gx < n_gx - 1).astype(jnp.int32)
     )
@@ -267,11 +269,13 @@
         def _():
             to_side(side, face_ref.at[side], gface_ref.at[1 - side], face_sem).start()
 
-    def fill(k, carry):
-        back_ref[k] = drag_ref[elem_ref[k]]
+    def fill(index, carry):
+        held = [drag_ref[elem_ref[index * 8 + u]] for u in range(8)]
+        for u in range(8):
+            back_ref[index * 8 + u] = held[u]
         return carry
 
-    lax.fori_loop(0, elems, fill, 0, unroll=4)
+    lax.fori_loop(0, elems // 8, fill, 0)
 
     def back_copy(off):
         peer = lax.rem(gy + off, n_gy)
@@ -284,11 +288,8 @@
     for off in range(1, n_gy):
         back_copy(off).start()
 
-    def keep(k, carry):
-        ret_ref[gy * share + k] = back_ref[gy * share + k]
-        return carry
-
-    lax.fori_loop(0, share, keep, 0, unroll=4)
+    mine = pl.ds(gy * share, share)
+    ret_ref[mine] = back_ref[mine]
 
     for side in range(2):
         @pl.when(has[side])
@@ -475,11 +476,14 @@
             copies.append(pltpu.make_async_copy(buf_ref.at[c, x], out_ref.at[c, x], sem.at[c, x]))
             copies[-1].start()
 
-    def pick(b, carry):
-        drag_ref[b] = ret_ref[position_ref[b]]
+    def pick(index, carry):
+        held = [ret_ref[position_ref[index * 8 + u]] for u in range(8)]
+        for c in range(3):
+            rows = jnp.concatenate([h[c : c + 1] for h in held], axis=0)
+            drag_ref[c, pl.ds(pl.multiple_of(index * 8, 8), 8), :] = rows
         return carry
 
-    lax.fori_loop(0, ret_ref.shape[0], pick, 0, unroll=4)
+    lax.fori_loop(0, ret_ref.shape[0] // 8, pick, 0)
     for copy in copies:
         copy.wait()
 
@@ -488,13 +492,96 @@
     f32 = jnp.float32
     return pl.pallas_call(
         yz_pass,
-        out_shape=(jax.ShapeDtypeStruct(field.shape, f32), jax.ShapeDtypeStruct(ret.shape, f32)),
+        out_shape=(jax.ShapeDtypeStruct(field.shape, f32), jax.ShapeDtypeStruct((3, ret.shape[0], 128), f32)),
         in_specs=[pl.BlockSpec(memory_space=SMEM)] + [pl.BlockSpec(memory_space=VMEM)] * 4,
         out_specs=[pl.BlockSpec(memory_space=pl.ANY), pl.BlockSpec(memory_space=VMEM)],
         scratch_shapes=[pltpu.VMEM(field.shape, f32), pltpu.SemaphoreType.DMA(field.shape[:2])],
         compiler_params=pltpu.CompilerParams(vmem_limit_bytes=32 * 1024 * 1024),
         name="yzpass",
     )(position, field, far_lo, far_hi, ret)
+
+
+def send_kernel(
+    n_gy, sorting_ref, pos_ref, vel_ref, coef_ref, label_ref,
+    got_ref, got_label_ref, send_ref, sem, label_sem,
+):
+    share = pos_ref.shape[1] // n_gy
+    gy = lax.axis_index("gy")
+    mesh_id = pl.DeviceIdType.MESH
+    barrier = pltpu.get_barrier_semaphore()
+    for off in range(1, n_gy):
+        pl.semaphore_signal(
+            barrier, inc=1, device_id={"gy": lax.rem(gy + off, n_gy)}, device_id_type=mesh_id
+        )
+
+    def block_copy(off):
+        peer = lax.rem(gy + off, n_gy)
+        return pltpu.make_async_remote_copy(
+            src_ref=send_ref.at[pl.ds(peer * share, share)], dst_ref=got_ref.at[pl.ds(gy * share, share)],
+            send_sem=sem.at[0, off - 1], recv_sem=sem.at[1, off - 1],
+            device_id={"gy": peer}, device_id_type=mesh_id,
+        )
+
+    def label_copy(off):
+        peer = lax.rem(gy + off, n_gy)
+        return pltpu.make_async_remote_copy(
+            src_ref=label_ref.at[peer], dst_ref=got_label_ref.at[gy],
+            send_sem=label_sem.at[0, off - 1], recv_sem=label_sem.at[1, off - 1],
+            device_id={"gy": peer}, device_id_type=mesh_id,
+        )
+
+    def pack(dst, start):
+        def some(index, carry):
+            held = []
+            for u in range(4):
+                b = sorting_ref[start + index * 4 + u]
+                rows = [ref[c, pl.ds(b, 1), :] for ref in (pos_ref, vel_ref) for c in range(3)]
+                held.append(jnp.concatenate(rows + [coef_ref[b]], axis=0))
+            for u in range(4):
+                dst[start + index * 4 + u] = held[u]
+            return carry
+
+        lax.fori_loop(0, share // 4, some, 0)
+
+    order = sorted(range(1, n_gy), key=lambda off: -min(off, n_gy - off))
+    for place, off in enumerate(order):
+        pack(send_ref, lax.rem(gy + off, n_gy) * share)
+        if place == 0:
+            pl.semaphore_wait(barrier, n_gy - 1)
+            for other in order:
+                label_copy(other).start()
+        block_copy(off).start()
+    pack(got_ref, gy * share)
+    got_label_ref[gy] = label_ref[gy]
+    for off in order:
+        label_copy(off).wait()
+    for off in order:
+        block_copy(off).wait()
+
+
+def run_send(sorting, pos, vel, coef, label):
+    n_gy = lax.axis_size("gy")
+    elems = pos.shape[1]
+    f32 = jnp.float32
+    dma = pltpu.SemaphoreType.DMA
+    return pl.pallas_call(
+        functools.partial(send_kernel, n_gy),
+        out_shape=(
+            jax.ShapeDtypeStruct((elems, 8, 128), f32),
+            jax.ShapeDtypeStruct(label.shape, f32),
+        ),
+        in_specs=[pl.BlockSpec(memory_space=SMEM)] + [pl.BlockSpec(memory_space=VMEM)] * 4,
+        out_specs=[pl.BlockSpec(memory_space=VMEM)] * 2,
+        scratch_shapes=[
+            pltpu.VMEM((elems, 8, 128), f32),
+            dma((2, n_gy - 1)),
+            dma((2, n_gy - 1)),
+        ],
+        compiler_params=pltpu.CompilerParams(
+            vmem_limit_bytes=32 * 1024 * 1024, collective_id=1, has_side_effects=True
+        ),
+        name="migrate",
+    )(sorting, pos, vel, coef, label)
 
 
 def inverse_of(position):
@@ -513,18 +600,23 @@
     earlier = (dest[None, :] == dest[:, None]) & (ladder[None, :] < ladder[:, None])
     position = dest * share + jnp.sum(earlier.astype(jnp.int32), axis=1)
     sorting = inverse_of(position)
-    packed = jnp.concatenate([part_pos, part_vel, part_coef], axis=1)[sorting]
-    labels = (elem * 256 + counts)[sorting].astype(f32)
-    got = lax.all_to_all(packed, "gy", split_axis=0, concat_axis=0, tiled=True)
-    got_labels = lax.all_to_all(labels.reshape(devices, share), "gy", split_axis=0, concat_axis=0, tiled=True)
-    got_labels = got_labels.reshape(elems).astype(jnp.int32)
+    lanes = max(128, share)
+    tags = elem * 256 + counts
+    room = (position // share) * lanes + position % share
+    cells = jnp.arange(devices * lanes, dtype=jnp.int32)
+    label = jnp.sum(jnp.where(room[None, :] == cells[:, None], tags[None, :], 0), axis=1)
+    got, got_label = run_send(
+        sorting, part_pos.transpose(1, 0, 2), part_vel.transpose(1, 0, 2), part_coef,
+        label.astype(f32).reshape(devices, 1, lanes),
+    )
+    got_labels = got_label[:, 0, :share].reshape(elems).astype(jnp.int32)
     slot = inverse_of(got_labels // 256)
     field, far_lo, far_hi, ret = run_main(
         slot, got_labels % 256, got_labels // 256, got,
         velocity.reshape(3, elems, nodes), (exd, eyd, ez),
     )
     source, drag_out = run_yz(position, field, far_lo, far_hi, ret)
-    return (drag_out, source)
+    return (drag_out.transpose(1, 0, 2), source)
 
 
 def solution(mesh):

time: 60.9 us -> 52.2 us (0.86)
  Pallas kernels: 36.6 us -> 46.7 us
  waiting for transfers between devices: 7.62 us -> 0 us
  starting transfers between devices: 7.58 us -> 0 us
  local copies, waits for them, and re-layouts: 6.7 us -> 3.98 us
  other arithmetic: 1.36 us -> 0.59 us
    pallas_call x0 -> x1, Pallas kernels: none -> 9.29 us  [run_send(): pl.pallas_call(functools.partial(send_kernel, n_gy), out_shape=(jax.Shape...]
    all_to_all x2 -> x0, waiting for transfers between devices: 7.62 us -> none  [the longest x1 7.62 us: body(): got = lax.all_to_all(packed, 'gy', split_axis=0, concat_axis=0, tiled=True)]
    all_to_all x2 -> x0, starting transfers between devices: 7.58 us -> none  [the longest x1 3.86 us: body(): lax.all_to_all(labels.reshape(devices, share), 'gy', split_axis=0, concat...]
    gather x2 -> x0, local copies, waits for them, and re-layouts: 2.78 us -> none  [the longest x1 1.55 us: body(): packed = jnp.concatenate([part_pos, part_vel, part_coef], axis=1)[sorting]]
    reduce_sum x1, other arithmetic: 0.92 us -> 0.17 us  [body(): position = dest * share + jnp.sum(earlier.astype(jnp.int32), axis=1)]
    unnamed x17 -> x14, local copies, waits for them, and re-layouts: 3.17 us -> 3.9 us
    pallas_call x1, Pallas kernels: 7.5 us -> 8.17 us  [run_yz(): pl.pallas_call(yz_pass, out_shape=(jax.ShapeDtypeStruct(field.shape, f32)...]
    convert_element_type x2 -> x1, local copies, waits for them, and re-layouts: 0.75 us -> 0.08 us  [body(): got_labels = got_label[:, 0, :share].reshape(elems).astype(jnp.int32)]
  transfers between devices with their start and end apart: 2 -> 0, of which waited for: 1 -> 0; matrix products, arithmetic and copies ran while one was open for 4% -> 0% of each run, Pallas kernels for 0% -> 0%
where the time goes in v3:
time: 52.2 us; the launch traced here: 52 us
  Pallas kernels  46.7 us (89%)
  local copies, waits for them, and re-layouts  3.98 us (8%)
  between operations  0.7 us (1%)
  other arithmetic  0.59 us (1%)
    pallas_call x1, Pallas kernels, run_main(): pl.pallas_call(functools.partial(main_kernel, shape, chunks, n_gx, n_gy),...  29.3 us
    pallas_call x1, Pallas kernels, run_send(): pl.pallas_call(functools.partial(send_kernel, n_gy), out_shape=(jax.Shape...  9.29 us
    pallas_call x1, Pallas kernels, run_yz(): pl.pallas_call(yz_pass, out_shape=(jax.ShapeDtypeStruct(field.shape, f32)...  8.17 us
    unnamed x14, local copies, waits for them, and re-layouts  3.9 us

profile of v3, /device:TPU:17, one launch (start us, length us, event | category | flops | bytes accessed | tf_op | source)
XLA Modules:
  0.0 52.0 jit_solution(4906983804294673659)
XLA Ops:
  0.6 0.0 copy-start.4
  0.6 0.6 %copy-done.4 = s32[128]{0:T(128)S(1)} copy-done((s32[128]{0:T(128)S(1)}, s32[128]{0:T(128)}, u32[]{:S(2)}) %copy-start.4) | copy-done | bytes 536
  1.3 0.0 copy-start.5
  1.3 0.0 copy-start.6
  1.3 0.2 convert_reduce_fusion
  1.5 0.5 copy-done.5
  1.9 0.0 copy-done.6
  2.0 0.1 select_reduce_fusion.2.sorting_ref
  2.1 0.2 select_reduce_fusion
  2.2 0.0 copy-start
  2.3 0.9 %copy-done = f32[128,3,128]{2,0,1:T(8,128)S(1)} copy-done((f32[128,3,128]{2,0,1:T(8,128)S(1)}, f32[128,3,128]{2,0,1:T(8,128)}, u32[]{:S(2)}) %copy-start) | copy-done | bytes 196632
  3.2 0.0 copy-start.1
  3.2 0.9 %copy-done.1 = f32[128,3,128]{2,0,1:T(8,128)S(1)} copy-done((f32[128,3,128]{2,0,1:T(8,128)S(1)}, f32[128,3,128]{2,0,1:T(8,128)}, u32[]{:S(2)}) %copy-start.1) | copy-done | bytes 196632
  4.1 0.0 copy-start.2
  4.1 0.9 %copy-done.2 = f32[128,2,128]{2,1,0:T(2,128)S(1)} copy-done((f32[128,2,128]{2,1,0:T(2,128)S(1)}, f32[128,2,128]{2,1,0:T(2,128)}, u32[]{:S(2)}) %copy-start.2) | copy-done | bytes 131096
  5.0 0.0 copy-start.3
  5.0 9.3 %migrate.1 = (f32[128,8,128]{2,1,0:T(8,128)S(1)}, f32[4,1,128]{2,1,0:T(1,128)S(1)}) custom-call(s32[128]{0:T(128)S(1)} %select_reduce_fusion.2.sorting_ref, f32[3,128,128]{2,1,0:T(8,128)S(1)} %bitcast.5, f32[3,128,128]{2,1,0:T(8,128)S(1)} %bitcast.6, f32[128,2,128]{2,1,0:T(2,128)S(1)} %copy-done.2, f32[4,1,128]{2,1,0:T(1,128)S(1)} %bitcast.7), custom_call_target="tpu_custom_call" | custom-call | tf_op jit(solution)/shard_map/migrate/pallas_call | solution.py:567
  14.3 0.1 convert_element_type.30
  14.4 0.1 select_reduce_fusion.1.slot_ref
  14.5 0.0 copy-done.3
  14.5 29.3 %elements.1 = (f32[3,2,4,16,512]{4,3,2,1,0:T(8,128)S(1)}, f32[3,2,16,128]{3,2,1,0:T(8,128)S(1)}, f32[3,2,16,128]{3,2,1,0:T(8,128)S(1)}, f32[128,3,128]{2,1,0:T(4,128)S(1)}) custom-call(s32[128]{0:T(128)S(1)} %select_reduce_fusion.1.slot_ref, s32[128]{0:T(128)S(1)} %get-tuple-element.20.count_ref, s32[128]{0:T(128)S(1)} %get-tuple-element.21.elem_ref, ...), custom_call_target="tpu_custom_call" | custom-call | flops 200000000 | bytes 4000000 | tf_op jit(solution)/shard_map/elements/pallas_call | solution.py:406
  43.8 8.2 %yzpass.1 = (f32[3,2,4,16,512]{4,3,2,1,0:T(8,128)}, f32[3,128,128]{2,1,0:T(8,128)}) custom-call(s32[128]{0:T(128)S(1)} %get-tuple-element.19.position_ref, f32[3,2,4,16,512]{4,3,2,1,0:T(8,128)S(1)} %get-tuple-element.12.field_ref, f32[3,2,16,128]{3,2,1,0:T(8,128)S(1)} %get-tuple-element.13.far_lo_ref, f32[3,2,16,128]{3,2,1,0:T(8,128)S(1)} %get-tuple-element.14.far_hi_ref, ...), custom_call_target="tpu_custom_call" | custom-call | tf_op jit(solution)/shard_map/yzpass/pallas_call | solution.py:493
  (4 shorter events, 0.1 us)
Async XLA Ops:
  0.6 0.7 %copy-start.4 = (s32[128]{0:T(128)S(1)}, s32[128]{0:T(128)}, u32[]{:S(2)}) copy-start(s32[128]{0:T(128)} %param.12) | copy-start | bytes 1540
  1.3 0.7 %copy-start.5 = (s32[128]{0:T(128)S(1)}, s32[128]{0:T(128)}, u32[]{:S(2)}) copy-start(s32[128]{0:T(128)} %param.11) | copy-start | bytes 1540
  1.3 0.7 %copy-start.6 = (s32[128]{0:T(128)S(1)}, s32[128]{0:T(128)}, u32[]{:S(2)}) copy-start(s32[128]{0:T(128)} %param.13) | copy-start | bytes 1540
  2.2 0.9 %copy-start = (f32[128,3,128]{2,0,1:T(8,128)S(1)}, f32[128,3,128]{2,0,1:T(8,128)}, u32[]{:S(2)}) copy-start(f32[128,3,128]{2,0,1:T(8,128)} %param.8) | copy-start | bytes 589828
  3.2 0.9 %copy-start.1 = (f32[128,3,128]{2,0,1:T(8,128)S(1)}, f32[128,3,128]{2,0,1:T(8,128)}, u32[]{:S(2)}) copy-start(f32[128,3,128]{2,0,1:T(8,128)} %param.9) | copy-start | bytes 589828
  4.1 0.9 %copy-start.2 = (f32[128,2,128]{2,1,0:T(2,128)S(1)}, f32[128,2,128]{2,1,0:T(2,128)}, u32[]{:S(2)}) copy-start(f32[128,2,128]{2,1,0:T(2,128)} %coef_ref.1) | copy-start | bytes 393220
  5.0 9.5 %copy-start.3 = (bf16[3,2,4,16,512]{4,3,2,1,0:T(8,128)(2,1)S(1)}, bf16[3,2,4,16,512]{4,3,2,1,0:T(8,128)(2,1)}, u32[]{:S(2)}) copy-start(bf16[3,2,4,16,512]{4,3,2,1,0:T(8,128)(2,1)} %param.7) | copy-start | bytes 1179652

commit v4 on v3

--- a/solution.py
+++ b/solution.py
@@ -155,10 +155,10 @@
     elems = exd * eyd * ez
     columns = eyd * ez
     share = elems // n_gy
-    group = 4
+    wide = columns // chunks
+    group = min(8, wide)
     turns = columns // group
     per = turns // chunks
-    wide = columns // chunks
     half = columns // 2
     gx = lax.axis_index("gx")
     gy = lax.axis_index("gy")
@@ -296,17 +296,14 @@
         def _():
             from_side(side, pos_ref.at[side], gpos_ref.at[side], pos_sem).wait()
 
-        def ghost(index, carry):
-            @pl.when(lax.rem(index, per) == 0)
-            def _():
-                chunk = lax.div(index, per)
-                from_side(
-                    side, drag_ref.at[pl.ds(base[side] + chunk * wide, wide)],
-                    gdrag_ref.at[side, pl.ds(chunk * wide, wide)], drag_sem, chunk,
-                ).wait()
-
-            for g in range(group):
-                col = index * group + g
+        def ghost(chunk, carry):
+            from_side(
+                side, drag_ref.at[pl.ds(base[side] + chunk * wide, wide)],
+                gdrag_ref.at[side, pl.ds(chunk * wide, wide)], drag_sem, chunk,
+            ).wait()
+            sums = []
+            for g in range(wide):
+                col = chunk * wide + g
                 place = gpos_ref[side, col]
                 force = gdrag_ref[side, col]
                 r, s, t = (jnp.broadcast_to(place[d : d + 1], (8, 128)) for d in range(3))
@@ -314,12 +311,14 @@
                 rows = [(-force[c : c + 1]) * weight for c in range(3)]
                 add = project(jnp.concatenate(rows, axis=0), st_planes(s, t, nodes))
                 spot = pl.ds(pl.multiple_of((base[side] + col) * ROWS, 8), ROWS)
-                ts_ref[spot, :] = ts_ref[spot, :] + add
+                sums.append((spot, ts_ref[spot, :] + add))
+            for spot, value in sums:
+                ts_ref[spot, :] = value
             return carry
 
         @pl.when(has[side])
         def _():
-            lax.fori_loop(0, turns, ghost, 0)
+            lax.fori_loop(0, chunks, ghost, 0)
 
     for side in range(2):
         @pl.when(has[side])

time: 52.2 us -> 49.2 us (0.943)
  Pallas kernels: 46.7 us -> 43.8 us
    pallas_call x1, Pallas kernels: 29.3 us -> 26.3 us  [run_main(): pl.pallas_call(functools.partial(main_kernel, shape, chunks, n_gx, n_gy),...]
where the time goes in v4:
time: 49.2 us; the launch traced here: 49 us
  Pallas kernels  43.8 us (89%)
  local copies, waits for them, and re-layouts  3.98 us (8%)
  between operations  0.7 us (1%)
  other arithmetic  0.59 us (1%)
    pallas_call x1, Pallas kernels, run_main(): pl.pallas_call(functools.partial(main_kernel, shape, chunks, n_gx, n_gy),...  26.3 us
    pallas_call x1, Pallas kernels, run_send(): pl.pallas_call(functools.partial(send_kernel, n_gy), out_shape=(jax.Shape...  9.29 us
    pallas_call x1, Pallas kernels, run_yz(): pl.pallas_call(yz_pass, out_shape=(jax.ShapeDtypeStruct(field.shape, f32)...  8.17 us
    unnamed x14, local copies, waits for them, and re-layouts  3.9 us

profile of v4, /device:TPU:17, one launch (start us, length us, event | category | flops | bytes accessed | tf_op | source)
XLA Modules:
  0.0 49.0 jit_solution(4923529894473801961)
XLA Ops:
  0.6 0.0 copy-start.4
  0.6 0.6 %copy-done.4 = s32[128]{0:T(128)S(1)} copy-done((s32[128]{0:T(128)S(1)}, s32[128]{0:T(128)}, u32[]{:S(2)}) %copy-start.4) | copy-done | bytes 536
  1.3 0.0 copy-start.5
  1.3 0.0 copy-start.6
  1.3 0.2 convert_reduce_fusion
  1.5 0.5 copy-done.5
  1.9 0.0 copy-done.6
  2.0 0.1 select_reduce_fusion.2.sorting_ref
  2.1 0.2 select_reduce_fusion
  2.2 0.0 copy-start
  2.3 0.9 %copy-done = f32[128,3,128]{2,0,1:T(8,128)S(1)} copy-done((f32[128,3,128]{2,0,1:T(8,128)S(1)}, f32[128,3,128]{2,0,1:T(8,128)}, u32[]{:S(2)}) %copy-start) | copy-done | bytes 196632
  3.2 0.0 copy-start.1
  3.2 0.9 %copy-done.1 = f32[128,3,128]{2,0,1:T(8,128)S(1)} copy-done((f32[128,3,128]{2,0,1:T(8,128)S(1)}, f32[128,3,128]{2,0,1:T(8,128)}, u32[]{:S(2)}) %copy-start.1) | copy-done | bytes 196632
  4.1 0.0 copy-start.2
  4.1 0.9 %copy-done.2 = f32[128,2,128]{2,1,0:T(2,128)S(1)} copy-done((f32[128,2,128]{2,1,0:T(2,128)S(1)}, f32[128,2,128]{2,1,0:T(2,128)}, u32[]{:S(2)}) %copy-start.2) | copy-done | bytes 131096
  5.0 0.0 copy-start.3
  5.0 9.3 %migrate.1 = (f32[128,8,128]{2,1,0:T(8,128)S(1)}, f32[4,1,128]{2,1,0:T(1,128)S(1)}) custom-call(s32[128]{0:T(128)S(1)} %select_reduce_fusion.2.sorting_ref, f32[3,128,128]{2,1,0:T(8,128)S(1)} %bitcast.5, f32[3,128,128]{2,1,0:T(8,128)S(1)} %bitcast.6, f32[128,2,128]{2,1,0:T(2,128)S(1)} %copy-done.2, f32[4,1,128]{2,1,0:T(1,128)S(1)} %bitcast.7), custom_call_target="tpu_custom_call" | custom-call | tf_op jit(solution)/shard_map/migrate/pallas_call | solution.py:566
  14.3 0.1 convert_element_type.30
  14.4 0.1 select_reduce_fusion.1.slot_ref
  14.5 0.0 copy-done.3
  14.5 26.3 %elements.1 = (f32[3,2,4,16,512]{4,3,2,1,0:T(8,128)S(1)}, f32[3,2,16,128]{3,2,1,0:T(8,128)S(1)}, f32[3,2,16,128]{3,2,1,0:T(8,128)S(1)}, f32[128,3,128]{2,1,0:T(4,128)S(1)}) custom-call(s32[128]{0:T(128)S(1)} %select_reduce_fusion.1.slot_ref, s32[128]{0:T(128)S(1)} %get-tuple-element.20.count_ref, s32[128]{0:T(128)S(1)} %get-tuple-element.21.elem_ref, ...), custom_call_target="tpu_custom_call" | custom-call | flops 200000000 | bytes 4000000 | tf_op jit(solution)/shard_map/elements/pallas_call | solution.py:405
  40.9 8.2 %yzpass.1 = (f32[3,2,4,16,512]{4,3,2,1,0:T(8,128)}, f32[3,128,128]{2,1,0:T(8,128)}) custom-call(s32[128]{0:T(128)S(1)} %get-tuple-element.19.position_ref, f32[3,2,4,16,512]{4,3,2,1,0:T(8,128)S(1)} %get-tuple-element.12.field_ref, f32[3,2,16,128]{3,2,1,0:T(8,128)S(1)} %get-tuple-element.13.far_lo_ref, f32[3,2,16,128]{3,2,1,0:T(8,128)S(1)} %get-tuple-element.14.far_hi_ref, ...), custom_call_target="tpu_custom_call" | custom-call | tf_op jit(solution)/shard_map/yzpass/pallas_call | solution.py:492
  (4 shorter events, 0.1 us)
Async XLA Ops:
  0.6 0.7 %copy-start.4 = (s32[128]{0:T(128)S(1)}, s32[128]{0:T(128)}, u32[]{:S(2)}) copy-start(s32[128]{0:T(128)} %param.12) | copy-start | bytes 1540
  1.3 0.7 %copy-start.5 = (s32[128]{0:T(128)S(1)}, s32[128]{0:T(128)}, u32[]{:S(2)}) copy-start(s32[128]{0:T(128)} %param.11) | copy-start | bytes 1540
  1.3 0.7 %copy-start.6 = (s32[128]{0:T(128)S(1)}, s32[128]{0:T(128)}, u32[]{:S(2)}) copy-start(s32[128]{0:T(128)} %param.13) | copy-start | bytes 1540
  2.2 0.9 %copy-start = (f32[128,3,128]{2,0,1:T(8,128)S(1)}, f32[128,3,128]{2,0,1:T(8,128)}, u32[]{:S(2)}) copy-start(f32[128,3,128]{2,0,1:T(8,128)} %param.8) | copy-start | bytes 589828
  3.2 0.9 %copy-start.1 = (f32[128,3,128]{2,0,1:T(8,128)S(1)}, f32[128,3,128]{2,0,1:T(8,128)}, u32[]{:S(2)}) copy-start(f32[128,3,128]{2,0,1:T(8,128)} %param.9) | copy-start | bytes 589828
  4.1 0.9 %copy-start.2 = (f32[128,2,128]{2,1,0:T(2,128)S(1)}, f32[128,2,128]{2,1,0:T(2,128)}, u32[]{:S(2)}) copy-start(f32[128,2,128]{2,1,0:T(2,128)} %coef_ref.1) | copy-start | bytes 393220
  5.0 9.5 %copy-start.3 = (bf16[3,2,4,16,512]{4,3,2,1,0:T(8,128)(2,1)S(1)}, bf16[3,2,4,16,512]{4,3,2,1,0:T(8,128)(2,1)}, u32[]{:S(2)}) copy-start(bf16[3,2,4,16,512]{4,3,2,1,0:T(8,128)(2,1)} %param.7) | copy-start | bytes 1179652
